TPU v7x, 256 devices: a 4x2x16 block of a 4x16x16 slice. The times are simulated.
256 devices in a mesh: pb: 2 (over y), col: 32 (over z, core), row: 4 (over x).
Axes of the slice: x: 4, y: 2, z: 16, core: 2. Of those that a mesh axis runs over, the one named last changes fastest.
The devices are a block of a 4x16x16 slice.
Arguments:
- pair_density: bfloat16 [6144, 6144], P(('pb', 'col'), 'row'), parts along dimension 0, may hold values from -0.19921875 to 0.19921875
- band_pairs: int32 [2, 3072], replicated, may hold values from 0 to 255, as said below
- valence: float32 [256], replicated, may hold values from -12 to -2
- conduction: float32 [12], replicated, may hold values from 1 to 8
- wave_vectors: int32 [3, 12288], P(None, 'pb'), parts along dimension 1, may hold values from -6 to 6
- momentum: float32 [6], P('pb'), parts along dimension 0, may hold values from 0.3 to 0.7
- guess_scale: float32 [12288], P('pb'), parts along dimension 0, may hold values from 0.4 to 0.75
Outputs:
- epsilon: float32 [12288, 6144], P(('pb', 'row'), 'col'), parts along dimension 0
- inverse: float32 [12288, 6144], P(('pb', 'row'), 'col'), parts along dimension 0
There are 2 independent parts, one for each index of `pb`. A program takes and returns all parts, laid end to end along the dimension named above; an argument that names none is the same for every part. Nothing has to cross between parts.
Inputs may be any that keep to these rules, and one draw needn't show every extreme that they name: `band_pairs`: column p names a valence band below 256 in row 0 and a conduction band below 12 in row 1; every such pair of bands appears in exactly one column.
All inputs are finite; a program needn't handle non-finite values.
Results may differ from a plain program's by a relative error of at most 0.0036.
The roundings to bfloat16 on the way count: a program that leaves them out, or rounds other values in their place, can miss the bound.
Values may be sent and summed in bfloat16 or wider, within the bound.
A program may use at most 64 MiB of HBM per device.

v0:
```python
import math

import jax
import jax.numpy as jnp
from jax import lax
from jax.sharding import PartitionSpec as P


def copy_for_each(array, axis):
    copies = jnp.broadcast_to(array, (lax.axis_size(axis), *array.shape))
    return lax.all_to_all(copies, axis, split_axis=0, concat_axis=0, tiled=True)


def in_order(pieces, dim):
    lengths = list(pieces.shape[1:])
    lengths[dim] *= pieces.shape[0]
    return jnp.moveaxis(pieces, 0, dim).reshape(lengths)


def gathered_copies(array, axis, dim):
    pieces = copy_for_each(array, axis)
    return in_order(pieces, dim)


def lookup(indices, table):
    levels = jnp.arange(table.shape[0], dtype=jnp.int32)
    picked = indices[:, None] == levels[None, :]
    return jnp.sum(jnp.where(picked, table[None, :], 0.0), axis=1)


def on_device(pair_density, band_pairs, valence, conduction, wave_vectors, momentum, guess_scale):
    column_index = lax.axis_index("col")
    row_index = lax.axis_index("row")
    row_height = pair_density.shape[1]
    whole_width = row_height * lax.axis_size("row")
    strip_width = whole_width // lax.axis_size("col")
    valence_of = lookup(band_pairs[0], valence)
    conduction_of = lookup(band_pairs[1], conduction)
    weight = 4.0 / (valence_of - conduction_of)
    shifted = wave_vectors.astype(jnp.float32) + momentum[:, None]
    sqrt_all = jnp.sqrt(4.0 * math.pi / jnp.sum(shifted * shifted, axis=0))
    row_first = row_index * row_height
    column_first = column_index * strip_width
    sqrt_rows = lax.dynamic_slice_in_dim(sqrt_all, row_first, row_height, 0)
    sqrt_cols = lax.dynamic_slice_in_dim(sqrt_all, column_first, strip_width, 0)
    scale_rows = lax.dynamic_slice_in_dim(guess_scale, row_first, row_height, 0)
    scale_cols = lax.dynamic_slice_in_dim(guess_scale, column_first, strip_width, 0)
    panel_pairs = lax.all_gather(pair_density, "col", axis=0, tiled=True)
    owner = column_first // row_height
    offset = column_first % row_height
    own_slice = lax.dynamic_slice_in_dim(panel_pairs, offset, strip_width, 1)
    candidates = lax.all_gather(own_slice, "row", axis=1, tiled=True)
    strip_pairs = lax.dynamic_slice_in_dim(candidates, owner * strip_width, strip_width, 1)
    weighted = (weight[:, None] * panel_pairs.astype(jnp.float32)).astype(jnp.bfloat16)
    weighted_strip = (weight[:, None] * strip_pairs.astype(jnp.float32)).astype(jnp.bfloat16)
    chi_block = lax.dot_general(
        weighted, strip_pairs, (((0,), (0,)), ((), ())), preferred_element_type=jnp.float32
    )
    chi_rows = jnp.sum(weighted.astype(jnp.float32) * panel_pairs.astype(jnp.float32), axis=0)
    chi_cols = jnp.sum(weighted_strip.astype(jnp.float32) * strip_pairs.astype(jnp.float32), axis=0)
    global_rows = row_first + jnp.arange(row_height, dtype=jnp.int32)
    global_cols = column_first + jnp.arange(strip_width, dtype=jnp.int32)
    identity = (global_rows[:, None] == global_cols[None, :]).astype(jnp.float32)
    epsilon = identity - sqrt_rows[:, None] * chi_block * sqrt_cols[None, :]
    guess_rows = scale_rows / (1.0 - sqrt_rows * chi_rows * sqrt_rows)
    guess_cols = scale_cols / (1.0 - sqrt_cols * chi_cols * sqrt_cols)
    mixed = epsilon * guess_cols[None, :]
    mixed_b = mixed.astype(jnp.bfloat16)
    panel_mixed = lax.all_gather(mixed_b, "col", axis=1, tiled=True)
    strip_mixed = gathered_copies(mixed_b, "row", 0)
    square = jnp.dot(panel_mixed, strip_mixed, preferred_element_type=jnp.float32)
    square_b = square.astype(jnp.bfloat16)
    strip_square = gathered_copies(square_b, "row", 0)
    cube = jnp.dot(panel_mixed, strip_square, preferred_element_type=jnp.float32)
    inverse = guess_rows[:, None] * (4.0 * identity - 6.0 * mixed + 4.0 * square - cube)
    return (epsilon, inverse)


def solution(mesh):
    placed = (P(("pb", "col"), "row"), P(), P(), P(), P(None, "pb"), P("pb"), P("pb"))
    return jax.shard_map(
        on_device,
        mesh=mesh,
        in_specs=placed,
        out_specs=(P(("pb", "row"), "col"), P(("pb", "row"), "col")),
        check_vma=False,
    )
```

profile of v0, /device:TPU:40, one launch (start us, length us, event | category | flops | bytes accessed | tf_op | source)
XLA Modules:
  0.0 344.4 jit_solution(10228950458131673058)
XLA Ops:
  7.2 0.1 all-gather.4.cloned.1.call-start
  7.2 0.7 all-gather.4.cloned.1.call-update
  8.0 0.1 all-gather.6.cloned.1.call-start
  8.1 93.0 %all-gather.4.cloned.1.call-done = bf16[3072,1536]{1,0:T(8,128)(2,1)} async-done(((bf16[96,1536]{1,0:T(8,128)(2,1)}), bf16[3072,1536]{1,0:T(8,128)(2,1)}) %all-gather.4.cloned.1.call-update) | async-done | bytes 9437200 | tf_op jit(solution)/shard_map/all_gather | solution.py:48
  101.1 2.4 constant_dynamic-slice_fusion
  103.5 0.0 copy-start.1
  103.5 0.0 copy-start.3
  103.5 0.0 copy-start.2
  103.5 1.5 copy.18
  105.0 0.1 all-gather.6.cloned.1.call-update
  105.1 0.1 all-gather.8.cloned.1.call-start
  105.3 0.1 select_reduce_fusion.1
  105.4 0.1 multiply_reduce_fusion
  105.5 1.9 select_reduce_fusion
  107.5 6.2 %fusion.1 = f32[1536]{0:T(1024)S(1)} fusion(bf16[3072,1536]{1,0:T(8,128)(2,1)} %all-gather.4.cloned.1.call-done, f32[3072]{0:T(1024)S(1)} %subtract_divide_fusion), kind=kLoop, calls=%fused_computation.3 | loop fusion | flops 28310016 | bytes 9455616 | tf_op jit(solution)/shard_map/reduce_sum | solution.py:59
  113.7 0.8 fusion.20
  114.5 45.3 %all-gather.6.cloned.1.call-done = bf16[3072,768]{0,1:T(8,128)(2,1)} async-done(((bf16[3072,192]{0,1:T(8,128)(2,1)}), bf16[3072,768]{0,1:T(8,128)(2,1)}) %all-gather.6.cloned.1.call-update) | async-done | bytes 4718608 | tf_op jit(solution)/shard_map/all_gather | solution.py:52
  159.8 1.7 fusion.15
  161.5 0.8 fusion.22
  162.3 7.6 %multiply_convert_fusion = (bf16[1536,192]{0,1:T(8,128)(2,1)}, f32[1536,192]{0,1:T(8,128)}) fusion(f32[192]{0:T(256)S(1)} %get-tuple-element.4, f32[192]{0:T(256)S(1)} %get-tuple-element.5, bf16[3072,1536]{1,0:T(8,128)(2,1)} %all-gather.4.cloned.1.call-done, f32[3072]{0:T(1024)S(1)} %subtract_divide_fusion, ...), kind=kOutput, calls=%fused_computation.20 | convolution fusion | flops 1828159488 | bytes 12413188 | tf_op jit(solution)/shard_map/dot_general | solution.py:56
  169.9 0.1 all-gather.8.cloned.1.call-update
  170.0 1.2 broadcast_in_dim.47
  171.2 32.2 %all_to_all.10 = bf16[4,1536,192]{1,2,0:T(8,128)(2,1)S(1)} all-to-all(bf16[4,1536,192]{1,2,0:T(8,128)(2,1)S(1)} %broadcast_in_dim.47), channel_id=1, replica_groups=mesh['pb'=2,'col'=32,'row'=4] {'row'}, dimensions={0} | all-to-all | bytes 4718592 | tf_op jit(solution)/shard_map/all_to_all | solution.py:11
  203.4 0.3 copy.21
  203.7 82.3 %all-gather.8.cloned.1.call-done = bf16[1536,6144]{0,1:T(8,128)(2,1)} async-done(((bf16[1536,192]{0,1:T(8,128)(2,1)}), bf16[1536,6144]{0,1:T(8,128)(2,1)}) %all-gather.8.cloned.1.call-update) | async-done | bytes 18874384 | tf_op jit(solution)/shard_map/all_gather | solution.py:69
  286.0 11.4 %fusion.25 = (bf16[1536,192]{0,1:T(8,128)(2,1)S(1)}, f32[1536,192]{0,1:T(8,128)}) fusion(bf16[6144,192]{0,1:T(8,128)(2,1)S(1)} %bitcast.13, bf16[1536,6144]{0,1:T(8,128)(2,1)} %all-gather.8.cloned.1.call-done), kind=kOutput, calls=%fused_computation.38 | convolution fusion | flops 3624173568 | bytes 23003136 | tf_op jit(solution)/shard_map/dot_general | solution.py:71
  297.4 0.2 broadcast_in_dim.48
  297.6 33.7 %all_to_all.11 = bf16[4,1536,192]{1,2,0:T(8,128)(2,1)S(1)} all-to-all(bf16[4,1536,192]{1,2,0:T(8,128)(2,1)S(1)} %broadcast_in_dim.48), channel_id=1, replica_groups=mesh['pb'=2,'col'=32,'row'=4] {'row'}, dimensions={0} | all-to-all | bytes 4718592 | tf_op jit(solution)/shard_map/all_to_all | solution.py:11
  331.3 0.3 copy.22
  331.6 1.0 copy-done.5
  332.6 0.4 copy-done.6
  332.9 4.9 %fusion.13 = f32[1536,192]{0,1:T(8,128)} fusion(bf16[6144,192]{0,1:T(8,128)(2,1)S(1)} %bitcast.12, bf16[1536,6144]{0,1:T(8,128)(2,1)S(1)} %bitcast.17, f32[1536,192]{0,1:T(8,128)S(1)} %copy-done.6, f32[1536,192]{0,1:T(8,128)S(1)} %copy-done.5, f32[192]{0:T(256)S(1)} %get-tuple-element.4, f32[1536]{0:T(1024)S(1)} %get-tuple-element.2, ...), kind=kOutput, calls=%fused_computation.13 | convolution fusion | flops 3626532864 | bytes 24786432 | tf_op jit(solution)/shard_map/dot_general | solution.py:74
  (25 shorter events, 0.1 us)
Async XLA Ops:
  7.2 93.9 %all-gather.4.cloned.1.call-start = ((), (), s32[]{:S(2)}) async-start(), calls=%async_computation.2 | async-start | bytes 9732096 | tf_op jit(solution)/shard_map/all_gather | solution.py:48
  8.0 151.8 %all-gather.6.cloned.1.call-start = ((), (), s32[]{:S(2)}) async-start(), calls=%async_computation.3 | async-start | bytes 5898240 | tf_op jit(solution)/shard_map/all_gather | solution.py:52
  103.5 1.7 copy-start.1
  103.5 1.7 copy-start.4
  103.5 1.9 copy-start
  103.5 1.9 copy-start.3
  103.5 2.0 copy-start.2
  105.1 180.9 %all-gather.8.cloned.1.call-start = ((), (), s32[]{:S(2)}) async-start(), calls=%async_computation.4 | async-start | bytes 19464192 | tf_op jit(solution)/shard_map/all_gather | solution.py:69
  286.0 45.6 %slice-start = ((s8[18874368]{0:T(1024)(128)(4,1)}), s8[4194304]{0:T(1024)(128)(4,1)S(1)}, s32[]{:S(2)}) async-start(s8[18874368]{0:T(1024)(128)(4,1)} %bitcast.16), calls=%async_computation.5 | async-start | bytes 8388608
  286.0 45.6 %slice-start.1 = ((s8[18874368]{0:T(1024)(128)(4,1)}), s8[4194304]{0:T(1024)(128)(4,1)S(1)}, s32[]{:S(2)}) async-start(s8[18874368]{0:T(1024)(128)(4,1)} %bitcast.16), calls=%async_computation.6 | async-start | bytes 8388608
  286.0 45.6 %slice-start.2 = ((s8[18874368]{0:T(1024)(128)(4,1)}), s8[4194304]{0:T(1024)(128)(4,1)S(1)}, s32[]{:S(2)}) async-start(s8[18874368]{0:T(1024)(128)(4,1)} %bitcast.16), calls=%async_computation.7 | async-start | bytes 8388608
  286.0 45.6 %slice-start.3 = ((s8[18874368]{0:T(1024)(128)(4,1)}), s8[4194304]{0:T(1024)(128)(4,1)S(1)}, s32[]{:S(2)}) async-start(s8[18874368]{0:T(1024)(128)(4,1)} %bitcast.16), calls=%async_computation.8 | async-start | bytes 8388608
  297.5 34.1 %slice-start.4 = ((s8[18874368]{0:T(1024)(128)(4,1)}), s8[2097152]{0:T(1024)(128)(4,1)S(1)}, s32[]{:S(2)}) async-start(s8[18874368]{0:T(1024)(128)(4,1)} %bitcast.16), calls=%async_computation.9 | async-start | bytes 4194304
  331.3 1.3 copy-start.5
  331.3 1.6 copy-start.6
Sparse Core Ops, SparseCore 0:
  9.9 91.1 all-gather.3
  105.2 54.5 all-gather.5
  170.1 115.8 all-gather.7
where the time goes:
time: 346 us; the launch traced here: 344 us
  waiting for transfers between devices  221 us (64%)
  blocking collectives  66 us (19%)
  matrix products  23.9 us (7%)
  between operations  14.1 us (4%)
  other arithmetic  11.6 us (3%)
  local copies, waits for them, and re-layouts  7.24 us (2%)
    all_gather x1, waiting for transfers between devices, on_device(): panel_pairs = lax.all_gather(pair_density, 'col', axis=0, tiled=True)  93 us
    all_gather x1, waiting for transfers between devices, on_device(): panel_mixed = lax.all_gather(mixed_b, 'col', axis=1, tiled=True)  82.3 us
    all_to_all x2, blocking collectives, copy_for_each(): return lax.all_to_all(copies, axis, split_axis=0, concat_axis=0, tiled=True)  66 us
    all_gather x1, waiting for transfers between devices, on_device(): candidates = lax.all_gather(own_slice, 'row', axis=1, tiled=True)  45.3 us
    dot_general x1, matrix products, on_device(): jnp.dot(panel_mixed, strip_mixed, preferred_element_type=jnp.float32)  11.4 us
    dot_general x1, matrix products, on_device(): lax.dot_general(weighted, strip_pairs, (((0,), (0,)), ((), ())), preferre...  7.64 us
  transfers between devices with their start and end apart: 3, of which 3 were waited for; matrix products, arithmetic and copies ran while one was open for 3% of the time, Pallas kernels for 0%

commit v1 on v0

--- a/solution.py
+++ b/solution.py
@@ -4,22 +4,6 @@
 import jax.numpy as jnp
 from jax import lax
 from jax.sharding import PartitionSpec as P
-
-
-def copy_for_each(array, axis):
-    copies = jnp.broadcast_to(array, (lax.axis_size(axis), *array.shape))
-    return lax.all_to_all(copies, axis, split_axis=0, concat_axis=0, tiled=True)
-
-
-def in_order(pieces, dim):
-    lengths = list(pieces.shape[1:])
-    lengths[dim] *= pieces.shape[0]
-    return jnp.moveaxis(pieces, 0, dim).reshape(lengths)
-
-
-def gathered_copies(array, axis, dim):
-    pieces = copy_for_each(array, axis)
-    return in_order(pieces, dim)
 
 
 def lookup(indices, table):
@@ -62,16 +46,28 @@
     global_cols = column_first + jnp.arange(strip_width, dtype=jnp.int32)
     identity = (global_rows[:, None] == global_cols[None, :]).astype(jnp.float32)
     epsilon = identity - sqrt_rows[:, None] * chi_block * sqrt_cols[None, :]
-    guess_rows = scale_rows / (1.0 - sqrt_rows * chi_rows * sqrt_rows)
+    diagonal_rows = 1.0 - sqrt_rows * chi_rows * sqrt_rows
+    guess_rows = scale_rows / diagonal_rows
     guess_cols = scale_cols / (1.0 - sqrt_cols * chi_cols * sqrt_cols)
     mixed = epsilon * guess_cols[None, :]
     mixed_b = mixed.astype(jnp.bfloat16)
-    panel_mixed = lax.all_gather(mixed_b, "col", axis=1, tiled=True)
-    strip_mixed = gathered_copies(mixed_b, "row", 0)
-    square = jnp.dot(panel_mixed, strip_mixed, preferred_element_type=jnp.float32)
-    square_b = square.astype(jnp.bfloat16)
-    strip_square = gathered_copies(square_b, "row", 0)
-    cube = jnp.dot(panel_mixed, strip_square, preferred_element_type=jnp.float32)
+    mixed_diagonal = diagonal_rows * guess_rows
+    rounded_diagonal = mixed_diagonal.astype(jnp.bfloat16).astype(jnp.float32)
+    delta = guess_rows + (rounded_diagonal - mixed_diagonal)
+    inner = sqrt_rows * guess_rows
+
+    def times_mixed(block):
+        wide = block.astype(jnp.float32)
+        scaled = (inner[:, None] * wide).astype(jnp.bfloat16)
+        partial = jnp.dot(panel_pairs, scaled, preferred_element_type=jnp.float32)
+        total = lax.psum(partial.astype(jnp.bfloat16), "row")
+        spread = lax.dot_general(
+            weighted, total, (((0,), (0,)), ((), ())), preferred_element_type=jnp.float32
+        )
+        return delta[:, None] * wide - sqrt_rows[:, None] * spread
+
+    square = times_mixed(mixed_b)
+    cube = times_mixed(square.astype(jnp.bfloat16))
     inverse = guess_rows[:, None] * (4.0 * identity - 6.0 * mixed + 4.0 * square - cube)
     return (epsilon, inverse)
 

time: 346 us -> 318 us (0.919)
  blocking collectives: 66 us -> 0 us
  waiting for transfers between devices: 221 us -> 258 us
  matrix products: 23.9 us -> 29.3 us
    psum x0 -> x2, waiting for transfers between devices: none -> 119 us  [times_mixed(): total = lax.psum(partial.astype(jnp.bfloat16), 'row')]
    all_gather x1 -> x0, waiting for transfers between devices: 82.3 us -> none  [on_device(): panel_mixed = lax.all_gather(mixed_b, 'col', axis=1, tiled=True)]
    all_to_all x2 -> x0, blocking collectives: 66 us -> none  [copy_for_each(): return lax.all_to_all(copies, axis, split_axis=0, concat_axis=0, tiled=True)]
    dot_general x2 -> x4, matrix products: 16.3 us -> 22.8 us  [the longest x2 14.3 us: times_mixed(): lax.dot_general(weighted, total, (((0,), (0,)), ((), ())), preferred_elem...]
  transfers between devices with their start and end apart: 3 -> 4, of which waited for: 3 -> 4; matrix products, arithmetic and copies ran while one was open for 3% -> 3% of each run, Pallas kernels for 0% -> 0%
where the time goes in v1:
time: 318 us
  waiting for transfers between devices  258 us (81%)
  matrix products  29.3 us (9%)
  between operations  14 us (4%)
  other arithmetic  11.8 us (4%)
  local copies, waits for them, and re-layouts  4.54 us (1%)
    psum x2, waiting for transfers between devices, times_mixed(): total = lax.psum(partial.astype(jnp.bfloat16), 'row')  119 us
    all_gather x1, waiting for transfers between devices, on_device(): panel_pairs = lax.all_gather(pair_density, 'col', axis=0, tiled=True)  93 us
    all_gather x1, waiting for transfers between devices, on_device(): candidates = lax.all_gather(own_slice, 'row', axis=1, tiled=True)  44.8 us
    dot_general x2, matrix products, times_mixed(): lax.dot_general(weighted, total, (((0,), (0,)), ((), ())), preferred_elem...  14.3 us
    dot_general x2, matrix products, times_mixed(): partial = jnp.dot(panel_pairs, scaled, preferred_element_type=jnp.float32)  8.49 us
    dot_general x1, matrix products, on_device(): lax.dot_general(weighted, strip_pairs, (((0,), (0,)), ((), ())), preferre...  6.48 us
  transfers between devices with their start and end apart: 4, of which 4 were waited for; matrix products, arithmetic and copies ran while one was open for 3% of the time, Pallas kernels for 0%

profile of v1, /device:TPU:40, one launch (start us, length us, event | category | flops | bytes accessed | tf_op | source)
XLA Modules:
  0.0 317.6 jit_solution(16853335193049921923)
XLA Ops:
  7.2 0.1 all-gather.3.cloned.1.call-start
  7.2 0.7 all-gather.3.cloned.1.call-update
  8.0 0.1 all-gather.5.cloned.1.call-start
  8.1 93.0 %all-gather.3.cloned.1.call-done = bf16[3072,1536]{1,0:T(8,128)(2,1)} async-done(((bf16[96,1536]{1,0:T(8,128)(2,1)}), bf16[3072,1536]{1,0:T(8,128)(2,1)}) %all-gather.3.cloned.1.call-update) | async-done | bytes 9437200 | tf_op jit(solution)/shard_map/all_gather | solution.py:32
  101.1 2.4 constant_dynamic-slice_fusion
  103.5 1.5 copy.11
  105.0 0.0 copy-start.2
  105.0 0.1 all-gather.5.cloned.1.call-update
  105.0 0.1 all-reduce.3.cloned.1.call-start
  105.2 0.5 copy-done.1
  105.7 0.0 copy-done.4
  105.7 0.1 select_reduce_fusion.1
  105.8 0.0 copy-done
  105.9 0.0 copy-done.3
  105.9 0.1 multiply_reduce_fusion
  106.0 1.9 select_reduce_fusion
  108.0 6.2 %fusion.1 = f32[1536]{0:T(1024)S(1)} fusion(bf16[3072,1536]{1,0:T(8,128)(2,1)} %all-gather.3.cloned.1.call-done, f32[3072]{0:T(1024)S(1)} %subtract_divide_fusion), kind=kLoop, calls=%fused_computation.3 | loop fusion | flops 28310016 | bytes 9455616 | tf_op jit(solution)/shard_map/reduce_sum | solution.py:43
  114.2 0.8 subtract_add_fusion
  115.0 44.8 %all-gather.5.cloned.1.call-done = bf16[3072,768]{0,1:T(8,128)(2,1)} async-done(((bf16[3072,192]{0,1:T(8,128)(2,1)}), bf16[3072,768]{0,1:T(8,128)(2,1)}) %all-gather.5.cloned.1.call-update) | async-done | bytes 4718608 | tf_op jit(solution)/shard_map/all_gather | solution.py:36
  159.8 1.8 fusion.11
  161.6 0.8 fusion.24
  162.4 6.5 %fusion.5 = f32[1536,192]{0,1:T(8,128)S(1)} fusion(bf16[3072,768]{0,1:T(8,128)(2,1)} %all-gather.5.cloned.1.call-done, s32[]{:T(128)S(6)} %select_n.39, f32[192]{0:T(256)S(1)} %get-tuple-element.6, f32[1536]{0:T(1024)S(1)} %get-tuple-element.4, s32[1536]{0:T(1024)S(1)} %iota_add_fusion, s32[192]{0:T(256)S(1)} %iota_add_fusion.1, ...), kind=kOutput, calls=%fused_computation.16 | convolution fusion | flops 1827569664 | bytes 11822596 | tf_op jit(solution)/shard_map/dot_general | solution.py:40
  168.9 0.0 copy-start.5
  168.9 4.3 %fusion.2 = bf16[3072,192]{0,1:T(8,128)(2,1)} fusion(bf16[3072,1536]{1,0:T(8,128)(2,1)S(1)} %bitcast.11, f32[1536]{0:T(1024)S(1)} %mul.163, f32[1536,192]{0,1:T(8,128)S(1)} %fusion.5, f32[192]{0:T(256)S(1)} %get-tuple-element.5), kind=kOutput, calls=%fused_computation.6 | convolution fusion | flops 1814003712 | bytes 11803392 | tf_op jit(solution)/shard_map/dot_general | solution.py:62
  173.2 0.1 all-reduce.3.cloned.1.call-update
  173.2 0.2 all-reduce.5.cloned.1.call-start
  173.5 59.1 %all-reduce.3.cloned.1.call-done = bf16[3072,192]{0,1:T(8,128)(2,1)} async-done(((bf16[3072,192]{0,1:T(8,128)(2,1)}), bf16[3072,192]{0,1:T(8,128)(2,1)}) %all-reduce.3.cloned.1.call-update) | async-done | bytes 1179664 | tf_op jit(solution)/shard_map/psum | solution.py:63
  232.6 6.5 %fusion.6 = f32[1536,192]{0,1:T(8,128)S(1)} fusion(bf16[3072,192]{0,1:T(8,128)(2,1)} %all-reduce.3.cloned.1.call-done, f32[1536]{0:T(1024)S(1)} %get-tuple-element.2, f32[1536]{0:T(1024)S(1)} %get-tuple-element.4, f32[1536,192]{0,1:T(8,128)S(1)} %fusion.5, f32[192]{0:T(256)S(1)} %get-tuple-element.5, bf16[3072,1536]{1,0:T(8,128)(2,1)} %all-gather.3.cloned.1.call-done, ...), kind=kOutput, calls=%fused_computation.17 | convolution fusion | flops 1827864576 | bytes 13001472 | tf_op jit(solution)/shard_map/dot_general | solution.py:64
  239.1 4.2 %fusion.3 = bf16[3072,192]{0,1:T(8,128)(2,1)} fusion(bf16[3072,1536]{1,0:T(8,128)(2,1)S(1)} %bitcast.13, f32[1536]{0:T(1024)S(1)} %mul.163, f32[1536,192]{0,1:T(8,128)S(1)} %fusion.6), kind=kOutput, calls=%fused_computation.7 | convolution fusion | flops 1813708800 | bytes 11802624 | tf_op jit(solution)/shard_map/dot_general | solution.py:62
  243.3 0.1 all-reduce.5.cloned.1.call-update
  243.4 59.8 %all-reduce.5.cloned.1.call-done = bf16[3072,192]{0,1:T(8,128)(2,1)} async-done(((bf16[3072,192]{0,1:T(8,128)(2,1)}), bf16[3072,192]{0,1:T(8,128)(2,1)}) %all-reduce.5.cloned.1.call-update) | async-done | bytes 1179664 | tf_op jit(solution)/shard_map/psum | solution.py:63
  303.2 7.8 %fusion.9 = f32[1536,192]{0,1:T(8,128)} fusion(bf16[3072,192]{0,1:T(8,128)(2,1)} %all-reduce.5.cloned.1.call-done, f32[1536,192]{0,1:T(8,128)S(1)} %fusion.6, f32[1536,192]{0,1:T(8,128)S(1)} %fusion.5, f32[1536]{0:T(1024)S(1)} %get-tuple-element.2, f32[192]{0:T(256)S(1)} %get-tuple-element.5, f32[1536]{0:T(1024)S(1)} %get-tuple-element.3, ...), kind=kOutput, calls=%fused_computation.20 | convolution fusion | flops 1830223872 | bytes 14194176 | tf_op jit(solution)/shard_map/dot_general | solution.py:64
  (26 shorter events, 0.1 us)
Async XLA Ops:
  7.2 93.9 %all-gather.3.cloned.1.call-start = ((), (), s32[]{:S(2)}) async-start(), calls=%async_computation | async-start | bytes 9732096 | tf_op jit(solution)/shard_map/all_gather | solution.py:32
  8.0 151.8 %all-gather.5.cloned.1.call-start = ((), (), s32[]{:S(2)}) async-start(), calls=%async_computation.1 | async-start | bytes 5898240 | tf_op jit(solution)/shard_map/all_gather | solution.py:36
  105.0 0.7 copy-start.1
  105.0 0.8 copy-start.4
  105.0 0.9 copy-start
  105.0 0.9 copy-start.3
  105.0 1.1 copy-start.2
  105.0 127.5 %all-reduce.3.cloned.1.call-start = ((), (), s32[]{:S(2)}) async-start(), calls=%async_computation.2 | async-start | bytes 2359296 | tf_op jit(solution)/shard_map/psum | solution.py:63
  159.8 9.1 %slice-start = ((s8[9437184]{0:T(1024)(128)(4,1)}), s8[4194304]{0:T(1024)(128)(4,1)S(1)}, s32[]{:S(2)}) async-start(s8[9437184]{0:T(1024)(128)(4,1)} %bitcast.10), calls=%async_computation.4 | async-start | bytes 8388608
  162.4 6.5 %slice-start.1 = ((s8[9437184]{0:T(1024)(128)(4,1)}), s8[4194304]{0:T(1024)(128)(4,1)S(1)}, s32[]{:S(2)}) async-start(s8[9437184]{0:T(1024)(128)(4,1)} %bitcast.10), calls=%async_computation.5 | async-start | bytes 8388608
  162.4 6.5 %slice-start.2 = ((s8[9437184]{0:T(1024)(128)(4,1)}), s8[1048576]{0:T(1024)(128)(4,1)S(1)}, s32[]{:S(2)}) async-start(s8[9437184]{0:T(1024)(128)(4,1)} %bitcast.10), calls=%async_computation.6 | async-start | bytes 2097152
  168.9 134.4 %copy-start.5 = (f32[1536,192]{0,1:T(8,128)}, f32[1536,192]{0,1:T(8,128)S(1)}, u32[]{:S(2)}) copy-start(f32[1536,192]{0,1:T(8,128)S(1)} %fusion.5) | copy-start | bytes 3538948
  173.2 65.9 %slice-start.3 = ((s8[9437184]{0:T(1024)(128)(4,1)}), s8[1048576]{0:T(1024)(128)(4,1)S(1)}, s32[]{:S(2)}) async-start(s8[9437184]{0:T(1024)(128)(4,1)} %bitcast.12), calls=%async_computation.7 | async-start | bytes 2097152
  173.2 130.0 %all-reduce.5.cloned.1.call-start = ((), (), s32[]{:S(2)}) async-start(), calls=%async_computation.3 | async-start | bytes 2359296 | tf_op jit(solution)/shard_map/psum | solution.py:63
  232.6 6.5 %slice-start.4 = ((s8[9437184]{0:T(1024)(128)(4,1)}), s8[4194304]{0:T(1024)(128)(4,1)S(1)}, s32[]{:S(2)}) async-start(s8[9437184]{0:T(1024)(128)(4,1)} %bitcast.12), calls=%async_computation.8 | async-start | bytes 8388608
  232.6 6.5 %slice-start.5 = ((s8[9437184]{0:T(1024)(128)(4,1)}), s8[4194304]{0:T(1024)(128)(4,1)S(1)}, s32[]{:S(2)}) async-start(s8[9437184]{0:T(1024)(128)(4,1)} %bitcast.12), calls=%async_computation.9 | async-start | bytes 8388608
Sparse Core Ops, SparseCore 0:
  9.9 91.1 all-gather.2
  105.2 54.5 all-gather.4
  173.4 59.1 all-reduce.2
  243.5 59.6 all-reduce.4

commit v2 on v1

v2 whole, which is shorter than its diff:
```python
import functools
import math

import jax
import jax.numpy as jnp
from jax import lax
from jax.experimental import pallas as pl
from jax.experimental.pallas import tpu as pltpu
from jax.sharding import PartitionSpec as P

MESH = pl.DeviceIdType.MESH
BF = jnp.bfloat16
F32 = jnp.float32
SUBS = 2


def lookup(indices, table):
    levels = jnp.arange(table.shape[0], dtype=jnp.int32)
    picked = indices[:, None] == levels[None, :]
    return jnp.sum(jnp.where(picked, table[None, :], 0.0), axis=1)


def mm(a, b, dims):
    return lax.dot_general(a, b, (dims, ((), ())), preferred_element_type=F32)


def kernel(ncol, nrow, pd, weights, rowv, colv, eps_out, inv_out,
           panel, wpan, strip, acc, chir, chic, rvec, cvec, sbuf, mixb, square, ybuf,
           keep, qsend, qrecv, qfull,
           ring_s, ring_r, pair_s, pair_r, sx_s, sx_r, sp_s, sp_r, own_s, loc_s, x_s, x_r):
    nz = ncol // 2
    half = nz // 2
    per = nz // nrow
    ch, height = pd.shape
    sub = ch // SUBS
    chip_wide = strip.shape[2]
    wide = chip_wide // 2
    hj = wide // 2
    pp = keep.shape[3]
    cpp = pp // ch
    col = lax.axis_index("col")
    x = lax.axis_index("row")
    z = col // 2
    core = lax.rem(col, 2)
    xr, xl = lax.rem(x + 1, nrow), lax.rem(x + nrow - 1, nrow)
    x2 = lax.rem(x + 2, nrow)
    up, down = lax.rem(col + 2, ncol), lax.rem(col + ncol - 2, ncol)
    mate = col + 1 - 2 * core
    home = z // per
    dist = lax.rem(x - home + nrow, nrow)
    lane0 = pl.multiple_of(lax.rem(z, per) * chip_wide, 128)

    def to(src, dst, ssem, rsem, **where):
        return pltpu.make_async_remote_copy(
            src_ref=src, dst_ref=dst, send_sem=ssem, recv_sem=rsem,
            device_id=where, device_id_type=MESH)

    barrier = pltpu.get_barrier_semaphore()
    for where in (dict(col=up), dict(col=down), dict(col=mate), dict(row=xr), dict(row=xl)):
        pl.semaphore_signal(barrier, inc=1, device_id=where, device_id_type=MESH)
    pl.semaphore_wait(barrier, 5)

    def chunk_of(d, s):
        away = jnp.where(d == 0, nz - s, s)
        return 2 * lax.rem(z + away, nz) + core

    def piece(ref, k, j):
        return ref.at[k, pl.ds(j * sub, sub)]

    def ring(d, s, j):
        k = chunk_of(d, s - 1)
        src = piece(panel, k, j)
        return to(src, piece(panel, k, j), ring_s.at[d, s - 1, j], ring_r.at[d, s - 1, j],
                  col=up if d == 0 else down)

    def ring_in(d, s, j):
        k = chunk_of(d, s)
        return to(piece(panel, k, j), piece(panel, k, j), ring_s.at[d, s - 1, j],
                  ring_r.at[d, s - 1, j], col=up)

    def pair(k, i, j):
        return to(piece(panel, k, j), piece(panel, k, j), pair_s.at[i, j], pair_r.at[i, j], col=mate)

    def cut(k, j):
        return panel.at[k, pl.ds(j * sub, sub), pl.ds(lane0, chip_wide)]

    def strip_first(k, i, j, side):
        return to(cut(k, j), piece(strip, k, j), sx_s.at[side, i, j], sx_r.at[i, j],
                  row=xr if side == 0 else xl)

    def strip_on(k, i, j, side):
        return to(piece(strip, k, j), piece(strip, k, j), sx_s.at[side, i, j], sx_r.at[i, j],
                  row=xr if side == 0 else xl)

    def strip_pair_first(k, i, j):
        return to(cut(k, j), piece(strip, k, j), sp_s.at[i, j], sp_r.at[i, j], col=mate)

    def strip_pair_on(k, i, j):
        return to(piece(strip, k, j), piece(strip, k, j), sp_s.at[i, j], sp_r.at[i, j], col=mate)

    def strip_local(k, i, j):
        return pltpu.make_async_copy(cut(k, j), piece(strip, k, j), loc_s.at[i, j])

    def place(d, s):
        return d * (half + 1) + s, chunk_of(d, s)

    def arrived(d, s, j):
        i, k = place(d, s)
        pair(k, i, j).start()

        @pl.when(dist == 0)
        def _():
            strip_first(k, i, j, 0).start()
            strip_first(k, i, j, 1).start()
            strip_pair_first(k, i, j).start()
            strip_local(k, i, j).start()

    def strip_step(d, s, j):
        i, k = place(d, s)

        @pl.when(dist != 0)
        def _():
            strip_on(k, i, j, 0).wait_recv()

        if d == 0:
            @pl.when(dist == 1)
            def _():
                strip_on(k, i, j, 0).start()
        else:
            @pl.when(dist == 3)
            def _():
                strip_on(k, i, j, 1).start()

        @pl.when(dist != 0)
        def _():
            strip_pair_on(k, i, j).start()

    def ready(d, s, j):
        i, k = place(d, s)
        km = k + 1 - 2 * core
        pair(km, i, j).wait_recv()
        strip_pair_on(km, i, j).wait_recv()

        @pl.when(dist == 0)
        def _():
            strip_local(k, i, j).wait()

    def work(zi):
        w0 = 2 * zi
        rows = 2 * ch
        wcol = weights[pl.ds(w0, 2)].reshape(rows, 128)
        for t in range(height // 128):
            lanes = slice(t * 128, (t + 1) * 128)
            pf = panel[pl.ds(w0, 2), :, lanes].reshape(rows, 128).astype(F32)
            wb = (pf * wcol).astype(BF)
            wpan[pl.ds(w0, 2), :, lanes] = wb.reshape(2, ch, 128)
            chir[:, lanes] += (wb.astype(F32) * pf).reshape(rows // 8, 8, 128).sum(0)
        for t in range(chip_wide // 128):
            lanes = slice(t * 128, (t + 1) * 128)
            sf = strip[pl.ds(w0, 2), :, lanes].reshape(rows, 128).astype(F32)
            wb = (sf * wcol).astype(BF).astype(F32)
            chic[:, lanes] += (wb * sf).reshape(rows // 8, 8, 128).sum(0)
        both = strip[pl.ds(w0, 2)].reshape(rows, chip_wide)
        mine = jnp.where(core == 0, both[:, :wide].astype(F32), both[:, wide:].astype(F32)).astype(BF)
        acc[...] += mm(mine, wpan[pl.ds(w0, 2)].reshape(rows, height), ((0,), (0,)))

    own = pltpu.make_async_copy(pd, panel.at[col], own_s)
    own.start()
    acc[...] = jnp.zeros_like(acc)
    chir[...] = jnp.zeros_like(chir)
    chic[...] = jnp.zeros_like(chic)
    own.wait()
    for j in range(SUBS):
        ring(0, 1, j).start()
        ring(1, 1, j).start()
    for j in range(SUBS):
        arrived(0, 0, j)

    def subs_of(d, last):
        if not last:
            return range(SUBS)
        return range(SUBS // 2) if d == 0 else range(SUBS // 2, SUBS)

    def bring(s, last, final):
        for j in range(SUBS):
            for d in (0, 1):
                if j in subs_of(d, final):
                    ring_in(d, s, j).wait_recv()
                    if not final:
                        if j in subs_of(d, last):
                            ring(d, s + 1, j).start()
                    arrived(d, s, j)

    def relay(s, final):
        for j in range(SUBS):
            for d in (0, 1):
                if j in subs_of(d, final):
                    strip_step(d, s, j)

    def settle(s, final):
        for j in range(SUBS):
            for d in (0, 1):
                if j in subs_of(d, final):
                    ready(d, s, j)

    bring(1, False, False)
    for j in range(SUBS):
        strip_step(0, 0, j)

    def early(s, carry):
        bring(s, False, False)
        relay(s - 1, False)

        @pl.when(s == 2)
        def _():
            for j in range(SUBS):
                ready(0, 0, j)

        @pl.when(s > 2)
        def _():
            settle(s - 2, False)

        def each(d, c):
            @pl.when((s > 2) | (d == 0))
            def _():
                work(chunk_of(d, s - 2) // 2)
            return c

        lax.fori_loop(0, 2, each, 0)
        return carry

    lax.fori_loop(2, half - 1, early, 0)
    def tail(s, final):
        settle(s, final)

        def each(d, c):
            work(chunk_of(d, s) // 2)
            return c
        lax.fori_loop(0, 1 if final else 2, each, 0)

    bring(half - 1, True, False)
    relay(half - 2, False)
    tail(half - 3, False)
    bring(half, False, True)
    relay(half - 1, False)
    tail(half - 2, False)
    relay(half, True)
    tail(half - 1, False)
    tail(half, True)

    s_r = rowv[0:1]
    chi_r = jnp.sum(chir[...], axis=0, keepdims=True)
    diag_r = 1.0 - s_r * chi_r * s_r
    g_r = rowv[1:2] / diag_r
    m_r = diag_r * g_r
    rvec[0:1] = g_r
    rvec[1:2] = g_r + (m_r.astype(BF).astype(F32) - m_r)
    rvec[2:3] = s_r * g_r
    chi_t = jnp.broadcast_to(jnp.sum(chic[...], axis=0, keepdims=True), chic.shape).T
    chi_c = jnp.where(core == 0, chi_t[:wide, 0:1], chi_t[wide:, 0:1])
    s_c = colv[:, 0:1]
    diag_c = 1.0 - s_c * chi_c * s_c
    g_c = colv[:, 1:2] / diag_c
    alpha = (diag_c * g_c).astype(BF).astype(F32)
    cvec[:, 0:1] = g_c
    cvec[:, 1:2] = alpha
    cvec[:, 2:3] = s_c * g_c * alpha
    cvec[:, 3:4] = s_c * g_c * alpha * alpha
    cvec[:, 4:5] = s_c

    def js(h):
        return slice(h * hj, (h + 1) * hj)

    def same(h):
        rows = lax.broadcasted_iota(jnp.int32, (hj, height), 1) + x * height
        cols = lax.broadcasted_iota(jnp.int32, (hj, height), 0) + (col * wide + h * hj)
        return rows == cols

    def begin(h):
        ident = same(h)
        e = jnp.where(ident, 1.0, 0.0) - rowv[0:1] * acc[js(h)] * cvec[js(h), 4:5]
        eps_out[js(h)] = e
        m = (e * cvec[js(h), 0:1]).astype(BF)
        mixb[js(h)] = m
        rest = m.astype(F32) - jnp.where(ident, cvec[js(h), 1:2], 0.0)
        sbuf[js(h)] = (rest * rvec[2:3]).astype(BF)

    def product(h):
        return (rvec[1:2] * mixb[js(h)].astype(F32)) - rowv[0:1] * ybuf[js(h)]

    def middle(h):
        sq = product(h) - (rowv[0:1] * acc[js(h)]) * cvec[js(h), 2:3]
        square[js(h)] = sq
        m = sq.astype(BF)
        mixb[js(h)] = m
        a = cvec[js(h), 1:2]
        rest = m.astype(F32) - jnp.where(same(h), a * a, 0.0)
        sbuf[js(h)] = (rest * rvec[2:3]).astype(BF)

    def finish(h):
        cube = product(h) - (rowv[0:1] * acc[js(h)]) * cvec[js(h), 3:4]
        mixed = eps_out[js(h)] * cvec[js(h), 0:1]
        four = jnp.where(same(h), 4.0, 0.0)
        inv_out[js(h)] = rvec[0:1] * (four - 6.0 * mixed + 4.0 * square[js(h)] - cube)

    def q_part(h, q, d):
        rows = panel[pl.ds((2 * q + d) * cpp, cpp)].reshape(pp, height)
        return mm(sbuf[js(h)], rows, ((1,), (1,)))

    def hop(u, i, src, dst, right):
        return to(src, dst, x_s.at[u, i], x_r.at[u, i], row=xr if right else xl)

    def slot(u, i, right):
        return hop(u, i, qsend.at[u, i], qrecv.at[u, i], right)

    def quarter(u, q, d):
        return qfull.at[u, q, :, pl.ds(d * pp, pp)]

    def gathered(u, i, q, d, right):
        return hop(u, i, quarter(u, q, d), quarter(u, q, d), right)

    def stage1(u, h):
        for i, q, d, right in ((0, x2, 0, False), (1, x2, 1, True), (2, xl, 1, False), (3, xr, 0, True)):
            qsend[u, i] = q_part(h, q, d).astype(BF)
            slot(u, i, right).start()
        for i, q, d in ((0, xl, 0), (1, xr, 1), (2, x, 0), (3, x, 1)):
            keep[h, i] = q_part(h, q, d)

    def stage2(u, h):
        for i, right in ((0, False), (1, True)):
            slot(u, i, right).wait_recv()
            qsend[u, 4 + i] = (keep[h, i] + qrecv[u, i].astype(F32)).astype(BF)
            slot(u, 4 + i, right).start()

    def stage3(u, h):
        for i in (2, 3):
            slot(u, i, True).wait_recv()
        for d in (0, 1):
            slot(u, 4 + d, True).wait_recv()
            direct = qrecv[u, 3 - d].astype(F32)
            total = keep[h, 2 + d] + direct + qrecv[u, 4 + d].astype(F32)
            qfull[u, x, :, d * pp:(d + 1) * pp] = total.astype(BF)
            gathered(u, 6 + d, x, d, True).start()
            gathered(u, 8 + d, x, d, False).start()

    def add(u, h, q, first):
        term = mm(qfull[u, q], wpan[pl.ds(2 * q * cpp, 2 * cpp)].reshape(2 * pp, height), ((1,), (0,)))
        if first:
            ybuf[js(h)] = term
        else:
            ybuf[js(h)] += term

    def stage4(u, h):
        add(u, h, x, True)
        gathered(u, 6, xl, 0, True).wait_recv()
        gathered(u, 10, xl, 0, True).start()
        gathered(u, 9, xr, 1, False).wait_recv()
        gathered(u, 11, xr, 1, False).start()
        gathered(u, 7, xl, 1, True).wait_recv()
        add(u, h, xl, False)
        gathered(u, 8, xr, 0, False).wait_recv()
        add(u, h, xr, False)

    def stage5(u, h):
        gathered(u, 10, x2, 0, True).wait_recv()
        gathered(u, 11, x2, 1, False).wait_recv()
        add(u, h, x2, False)

    for h in (0, 1):
        begin(h)
        stage1(h, h)
    for stage in (stage2, stage3, stage4):
        for h in (0, 1):
            stage(h, h)
    for h in (0, 1):
        stage5(h, h)
        middle(h)
        stage1(2 + h, h)
    for stage in (stage2, stage3, stage4):
        for h in (0, 1):
            stage(2 + h, h)
    for h in (0, 1):
        stage5(2 + h, h)
        finish(h)

    for u in range(4):
        for i in range(6):
            slot(u, i, True).wait_send()
        for i in range(6, 12):
            gathered(u, i, x, 0, True).wait_send()

    def drain(d, s, j):
        i, k = place(d, s)
        pair(k, i, j).wait_send()
        strip_pair_on(k, i, j).wait_send()

        @pl.when((dist == 0) | (dist == (1 if d == 0 else 3)))
        def _():
            strip_on(k, i, j, d).wait_send()

        @pl.when(dist == 0)
        def _():
            strip_on(k, i, j, 1 - d).wait_send()

    for j in range(SUBS):
        drain(0, 0, j)

        def each(s, carry):
            for d in (0, 1):
                ring(d, s, j).wait_send()
                drain(d, s, j)
            return carry

        lax.fori_loop(1, half, each, 0)
        for d in (0, 1):
            if j in subs_of(d, True):
                ring(d, half, j).wait_send()
                drain(d, half, j)


def on_device(ncol, nrow, pair_density, band_pairs, valence, conduction, wave_vectors, momentum, guess_scale):
    column_index = lax.axis_index("col")
    row_index = lax.axis_index("row")
    ch, height = pair_density.shape
    pairs = ch * ncol
    wide = height * nrow // ncol
    weight = 4.0 / (lookup(band_pairs[0], valence) - lookup(band_pairs[1], conduction))
    weights = jnp.broadcast_to(weight[:, None], (pairs, 128)).reshape(ncol, ch, 128)
    shifted = wave_vectors.astype(F32) + momentum[:, None]
    sqrt_all = jnp.sqrt(4.0 * math.pi / jnp.sum(shifted * shifted, axis=0))
    both = jnp.stack([sqrt_all, guess_scale])
    rowv = jnp.pad(lax.dynamic_slice_in_dim(both, row_index * height, height, 1), ((0, 6), (0, 0)))
    colv = jnp.pad(lax.dynamic_slice_in_dim(both, column_index * wide, wide, 1).T, ((0, 0), (0, 126)))
    half = ncol // 4
    places = 2 * (half + 1)
    hj = wide // 2
    pp = pairs // 8
    vm = pl.BlockSpec(memory_space=pltpu.VMEM)
    dma = pltpu.SemaphoreType.DMA
    out = jax.ShapeDtypeStruct((wide, height), F32)
    eps_t, inv_t = pl.pallas_call(
        functools.partial(kernel, ncol, nrow),
        out_shape=(out, out),
        in_specs=[vm] * 4,
        out_specs=(vm, vm),
        scratch_shapes=[
            pltpu.VMEM((ncol, ch, height), BF),
            pltpu.VMEM((ncol, ch, height), BF),
            pltpu.VMEM((ncol, ch, 2 * wide), BF),
            pltpu.VMEM((wide, height), F32),
            pltpu.VMEM((8, height), F32),
            pltpu.VMEM((8, 2 * wide), F32),
            pltpu.VMEM((8, height), F32),
            pltpu.VMEM((wide, 128), F32),
            pltpu.VMEM((wide, height), BF),
            pltpu.VMEM((wide, height), BF),
            pltpu.VMEM((wide, height), F32),
            pltpu.VMEM((wide, height), F32),
            pltpu.VMEM((2, 4, hj, pp), F32),
            pltpu.VMEM((4, 6, hj, pp), BF),
            pltpu.VMEM((4, 6, hj, pp), BF),
            pltpu.VMEM((4, nrow, hj, 2 * pp), BF),
            dma((2, half, SUBS)),
            dma((2, half, SUBS)),
            dma((places, SUBS)),
            dma((places, SUBS)),
            dma((2, places, SUBS)),
            dma((places, SUBS)),
            dma((places, SUBS)),
            dma((places, SUBS)),
            dma(()),
            dma((places, SUBS)),
            dma((4, 12)),
            dma((4, 12)),
        ],
        compiler_params=pltpu.CompilerParams(
            collective_id=0, has_side_effects=True, vmem_limit_bytes=60 * 1024 * 1024
        ),
        name="cohsex",
    )(pair_density, weights, rowv, colv)
    return eps_t.T, inv_t.T


def solution(mesh):
    placed = (P(("pb", "col"), "row"), P(), P(), P(), P(None, "pb"), P("pb"), P("pb"))
    return jax.shard_map(
        functools.partial(on_device, mesh.shape["col"], mesh.shape["row"]),
        mesh=mesh,
        in_specs=placed,
        out_specs=(P(("pb", "row"), "col"), P(("pb", "row"), "col")),
        check_vma=False,
    )
```

time: 318 us -> 151 us (0.47)
  waiting for transfers between devices: 258 us -> 0 us
  Pallas kernels: 0 us -> 137 us
  matrix products: 29.3 us -> 0 us
  between operations: 14 us -> 0.7 us
  other arithmetic: 11.8 us -> 5.9 us
    all_gather x2 -> x0, waiting for transfers between devices: 138 us -> none  [the longest x1 93 us: on_device(): panel_pairs = lax.all_gather(pair_density, 'col', axis=0, tiled=True)]
    pallas_call x0 -> x1, Pallas kernels: none -> 137 us  [on_device(): pl.pallas_call(functools.partial(kernel, ncol, nrow), out_shape=(out, out...]
    psum x2 -> x0, waiting for transfers between devices: 119 us -> none  [times_mixed(): total = lax.psum(partial.astype(jnp.bfloat16), 'row')]
    dot_general x5 -> x0, matrix products: 29.3 us -> none  [the longest x2 14.3 us: times_mixed(): lax.dot_general(weighted, total, (((0,), (0,)), ((), ())), preferred_elem...]
    reduce_sum x2 -> x0, other arithmetic: 8.02 us -> none  [the longest x1 6.21 us: on_device(): jnp.sum(weighted.astype(jnp.float32) * panel_pairs.astype(jnp.float32), a...]
    dynamic_slice x2 -> x0, local copies, waits for them, and re-layouts: 3.91 us -> none  [on_device(): own_slice = lax.dynamic_slice_in_dim(panel_pairs, offset, strip_width, 1)]
  transfers between devices with their start and end apart: 4 -> 0, of which waited for: 4 -> 0; matrix products, arithmetic and copies ran while one was open for 3% -> 0% of each run, Pallas kernels for 0% -> 0%
where the time goes in v2:
time: 151 us
  Pallas kernels  137 us (91%)
  local copies, waits for them, and re-layouts  7.4 us (5%)
  other arithmetic  5.9 us (4%)
    pallas_call x1, Pallas kernels, on_device(): pl.pallas_call(functools.partial(kernel, ncol, nrow), out_shape=(out, out...  137 us
    unnamed x5, local copies, waits for them, and re-layouts  3.59 us
    reduce_sum x2, other arithmetic, lookup(): return jnp.sum(jnp.where(picked, table[None, :], 0.0), axis=1)  3.31 us

profile of v2, /device:TPU:40, one launch (start us, length us, event | category | flops | bytes accessed | tf_op | source)
XLA Modules:
  0.0 150.6 jit_solution(19975142281072886)
XLA Ops:
  0.6 1.0 multiply_reduce_fusion
  1.7 0.8 fusion.1
  2.5 0.8 fusion
  3.2 0.8 fusion.2
  4.1 0.8 select_reduce_fusion.1
  4.9 2.5 %select_reduce_fusion = f32[3072]{0:T(1024)S(1)} fusion(f32[256]{0:T(256)} %param.9, s32[3072]{0:T(1024)S(1)} %bitcast.14), kind=kLoop, calls=%fused_computation | loop fusion | flops 2356224 | bytes 25600 | tf_op jit(solution)/shard_map/reduce_sum | solution.py:20
  7.4 0.1 div.29
  7.5 0.6 pad.8.rowv
  8.1 0.1 copy.15
  8.2 0.7 pad.9.colv
  8.9 1.6 %broadcast_in_dim.39.weights = f32[32,96,128]{2,1,0:T(8,128)} broadcast(f32[32,96]{1,0:T(8,128)S(1)} %div.29), dimensions={0,1} | broadcast | bytes 1585152 | tf_op jit(solution)/shard_map/broadcast_in_dim | solution.py:428
  10.5 136.5 %cohsex.1 = (f32[192,1536]{1,0:T(8,128)}, f32[192,1536]{1,0:T(8,128)}) custom-call(bf16[96,1536]{1,0:T(8,128)(2,1)} %pd.1, f32[32,96,128]{2,1,0:T(8,128)} %broadcast_in_dim.39.weights, f32[8,1536]{1,0:T(8,128)} %pad.8.rowv, f32[192,128]{1,0:T(8,128)} %pad.9.colv), custom_call_target="tpu_custom_call" | custom-call | tf_op jit(solution)/shard_map/cohsex/pallas_call | solution.py:441
  147.1 0.0 copy-start
  147.1 2.5 %copy.18 = f32[1536,192]{0,1:T(8,128)} copy(f32[1536,192]{0,1:T(8,128)} %bitcast.8) | data formatting | bytes 2359296
  149.5 0.0 copy-done
  149.5 1.0 copy.19
  (2 shorter events, 0.0 us)
Async XLA Ops:
  147.1 2.5 %copy-start = (f32[192,1536]{1,0:T(8,128)S(1)}, f32[192,1536]{1,0:T(8,128)}, u32[]{:S(2)}) copy-start(f32[192,1536]{1,0:T(8,128)} %get-tuple-element.5) | copy-start | bytes 3538948

commit v3 on v2

v3 whole, which is shorter than its diff:
```python
import functools
import math

import jax
import jax.numpy as jnp
from jax import lax
from jax.experimental import pallas as pl
from jax.experimental.pallas import tpu as pltpu
from jax.sharding import PartitionSpec as P

MESH = pl.DeviceIdType.MESH
BF = jnp.bfloat16
F32 = jnp.float32
SUBS = 2


def mm(a, b, dims):
    return lax.dot_general(a, b, (dims, ((), ())), preferred_element_type=F32)


def kernel(ncol, nrow, pd, bands, wave, scale, valence, conduction, momentum,
           eps_out, inv_out,
           panel, wpan, strip, weights, acc, chir, chic, rvec, cvec, sbuf, mixb, square, ybuf,
           keep, qsend, qrecv, qfull,
           ring_s, ring_r, pair_s, pair_r, sx_s, sx_r, sp_s, sp_r, own_s, loc_s, x_s, x_r,
           hello, cross, known):
    nz = ncol // 2
    half = nz // 2
    per = nz // nrow
    ch, height = pd.shape
    sub = ch // SUBS
    chip_wide = strip.shape[3]
    wide = chip_wide // 2
    hj = wide // 2
    pp = keep.shape[3]
    czp = pp // ch // 2
    meet, share = half // 2 - 1, half - 2
    col = lax.axis_index("col")
    x = lax.axis_index("row")
    z = col // 2
    core = lax.rem(col, 2)
    other = 1 - core
    xr, xl = lax.rem(x + 1, nrow), lax.rem(x + nrow - 1, nrow)
    x2 = lax.rem(x + 2, nrow)
    up, down = lax.rem(col + 2, ncol), lax.rem(col + ncol - 2, ncol)
    mate = col + 1 - 2 * core
    home = z // per
    dist = lax.rem(x - home + nrow, nrow)
    lane0 = pl.multiple_of(lax.rem(z, per) * chip_wide, 128)
    odd = lax.rem(z + x, 2)
    near = (dict(col=up), dict(col=down), dict(row=xr), dict(row=xl))

    def to(src, dst, ssem, rsem, **where):
        return pltpu.make_async_remote_copy(
            src_ref=src, dst_ref=dst, send_sem=ssem, recv_sem=rsem,
            device_id=where, device_id_type=MESH)

    def tell(sem, where):
        pl.semaphore_signal(sem, inc=1, device_id=where, device_id_type=MESH)

    barrier = pltpu.get_barrier_semaphore()

    @pl.when(odd == 1)
    def _():
        for where in near:
            tell(barrier, where)
        tell(barrier, dict(col=mate))

    @pl.when(odd == 0)
    def _():
        pl.semaphore_wait(barrier, 4)
        for where in near:
            tell(hello, where)

    @pl.when(odd == 1)
    def _():
        pl.semaphore_wait(hello, 4)

    def mate_first():
        @pl.when(odd == 1)
        def _():
            pl.semaphore_wait(barrier, 1)
            tell(cross, dict(col=mate))

    def mate_second():
        @pl.when(odd == 1)
        def _():
            pl.semaphore_wait(cross, 1)
            tell(known, dict(col=down))

        @pl.when(odd == 0)
        def _():
            pl.semaphore_wait(known, 1)

    def z_of(d, s):
        return lax.rem(z + jnp.where(d == 0, nz - s, s), nz)

    def piece(ref, k, j):
        return ref.at[k, core, pl.ds(j * sub, sub)]

    def ring(d, s, j):
        src = piece(panel, z_of(d, s - 1), j)
        return to(src, src, ring_s.at[d, s - 1, j], ring_r.at[d, s - 1, j],
                  col=up if d == 0 else down)

    def ring_in(d, s, j):
        dst = piece(panel, z_of(d, s), j)
        return to(dst, dst, ring_s.at[d, s - 1, j], ring_r.at[d, s - 1, j], col=up)

    def pair(k, c, i):
        return to(panel.at[k, c], panel.at[k, c], pair_s.at[i], pair_r.at[i], col=mate)

    def strip_pair(k, c, i):
        return to(strip.at[k, c], strip.at[k, c], sp_s.at[i], sp_r.at[i], col=mate)

    def cut(k, j):
        return panel.at[k, core, pl.ds(j * sub, sub), pl.ds(lane0, chip_wide)]

    def strip_hop(k, i, j, side, first):
        return to(cut(k, j) if first else piece(strip, k, j), piece(strip, k, j),
                  sx_s.at[side, i, j], sx_r.at[i, j], row=xr if side == 0 else xl)

    def strip_local(k, i, j):
        return pltpu.make_async_copy(cut(k, j), piece(strip, k, j), loc_s.at[i, j])

    def place(d, s):
        return d * (half + 1) + s, z_of(d, s)

    def arrived(d, s, j):
        i, k = place(d, s)

        @pl.when(dist == 0)
        def _():
            strip_hop(k, i, j, 0, True).start()
            strip_hop(k, i, j, 1, True).start()
            strip_local(k, i, j).start()

    def strip_step(d, s, j):
        i, k = place(d, s)

        @pl.when(dist == 0)
        def _():
            strip_local(k, i, j).wait()

        @pl.when(dist != 0)
        def _():
            strip_hop(k, i, j, 0, False).wait_recv()

        @pl.when(dist == (1 if d == 0 else 3))
        def _():
            strip_hop(k, i, j, d, False).start()

    def give(d, s):
        i, k = place(d, s)
        pair(k, core, i).start()
        strip_pair(k, core, i).start()

    def take(d, s):
        i, k = place(d, s)
        pair(k, other, i).wait_recv()
        strip_pair(k, other, i).wait_recv()

    def work(za, zb, c):
        def one(n, carry):
            k = jnp.where(n == 0, za, zb)
            wcol = weights[pl.ds(pl.multiple_of((2 * k + c) * ch, 8), ch)]
            for t in range(height // 128):
                lanes = slice(t * 128, (t + 1) * 128)
                pf = panel[k, c, :, lanes].astype(F32)
                wb = (pf * wcol).astype(BF)
                wpan[k, c, :, lanes] = wb
                chir[:, lanes] += (wb.astype(F32) * pf).reshape(ch // 8, 8, 128).sum(0)
            for t in range(chip_wide // 128):
                lanes = slice(t * 128, (t + 1) * 128)
                sf = strip[k, c, :, lanes].astype(F32)
                wb = (sf * wcol).astype(BF).astype(F32)
                chic[:, lanes] += (wb * sf).reshape(ch // 8, 8, 128).sum(0)
            return carry

        lax.fori_loop(0, 2, one, 0)
        both = jnp.concatenate([strip[za, c], strip[zb, c]], axis=0)
        mine = jnp.where(core == 0, both[:, :wide].astype(F32), both[:, wide:].astype(F32)).astype(BF)
        acc[...] += mm(mine, jnp.concatenate([wpan[za, c], wpan[zb, c]], axis=0), ((0,), (0,)))

    own = pltpu.make_async_copy(pd, panel.at[z, core], own_s)
    own.start()
    own.wait()
    for j in range(SUBS):
        ring(0, 1, j).start()
        ring(1, 1, j).start()
    for j in range(SUBS):
        arrived(0, 0, j)
    acc[...] = jnp.zeros_like(acc)
    chir[...] = jnp.zeros_like(chir)
    chic[...] = jnp.zeros_like(chic)

    def look(ids, table):
        def level(v, found):
            return jnp.where(ids == v, table[v], found)
        return lax.fori_loop(0, table.shape[0], level, jnp.zeros(ids.shape, F32), unroll=4)

    weight = 4.0 / (look(bands[0:1], valence) - look(bands[1:2], conduction))
    for t in range(weights.shape[0] // 128):
        lanes = slice(t * 128, (t + 1) * 128)
        weights[lanes] = jnp.broadcast_to(weight[:, lanes], (128, 128)).T

    def subs_of(d, last):
        if not last:
            return range(SUBS)
        return range(SUBS // 2) if d == 0 else range(SUBS // 2, SUBS)

    def bring(s, last, final):
        for j in range(SUBS):
            for d in (0, 1):
                if j in subs_of(d, final):
                    ring_in(d, s, j).wait_recv()
                    if not final and j in subs_of(d, last):
                        ring(d, s + 1, j).start()
                    arrived(d, s, j)

    def relay(s, final):
        for j in range(SUBS):
            for d in (0, 1):
                if j in subs_of(d, final):
                    strip_step(d, s, j)

    def unit(s, c):
        work(z_of(0, s), z_of(1, s), c)

    bring(1, False, False)
    for j in range(SUBS):
        strip_step(0, 0, j)

    def step(s, carry):
        bring(s, False, False)
        relay(s - 1, False)

        @pl.when(s == meet)
        def _():
            mate_first()

        @pl.when(s == share)
        def _():
            mate_second()
            give(0, 0)

            def bulk(r, c):
                give(0, r)
                give(1, r)
                return c
            lax.fori_loop(1, share, bulk, 0)

        unit(s - 1, core)
        return carry

    if meet < 2:
        mate_first()
    lax.fori_loop(2, half - 1, step, 0)
    bring(half - 1, True, False)
    relay(half - 2, False)
    give(0, half - 2)
    give(1, half - 2)
    unit(half - 2, core)
    bring(half, False, True)
    relay(half - 1, False)
    give(0, half - 1)
    give(1, half - 1)
    unit(half - 1, core)
    relay(half, True)
    give(0, half)
    work(z, z_of(0, half), core)

    def mates(s, carry):
        take(0, s)
        take(1, s)
        unit(s, other)
        return carry

    lax.fori_loop(1, half, mates, 0)
    take(0, 0)
    take(0, half)
    work(z, z_of(0, half), other)

    def root(first, count):
        lanes = pl.ds(pl.multiple_of(first, 128), count)
        total = jnp.zeros((1, count), F32)
        for i in range(3):
            shifted = wave[i:i + 1, lanes].astype(F32) + momentum[i]
            total = total + shifted * shifted
        return jnp.sqrt(4.0 * math.pi / total), scale[:, lanes]

    s_r, t_r = root(x * height, height)
    chi_r = jnp.sum(chir[...], axis=0, keepdims=True)
    diag_r = 1.0 - s_r * chi_r * s_r
    g_r = t_r / diag_r
    m_r = diag_r * g_r
    rvec[0:1] = g_r
    rvec[1:2] = g_r + (m_r.astype(BF).astype(F32) - m_r)
    rvec[2:3] = s_r * g_r
    rvec[3:4] = s_r
    s_l, t_l = root(z * chip_wide, chip_wide)
    chi_l = jnp.sum(chic[...], axis=0, keepdims=True)
    chic[0:1] = s_l
    chic[1:2] = t_l
    chic[2:3] = chi_l
    turned = chic[...].T
    turned = jnp.where(core == 0, turned[:wide], turned[wide:])
    s_c = turned[:, 0:1]
    diag_c = 1.0 - s_c * turned[:, 2:3] * s_c
    g_c = turned[:, 1:2] / diag_c
    alpha = (diag_c * g_c).astype(BF).astype(F32)
    cvec[:, 0:1] = g_c
    cvec[:, 1:2] = alpha
    cvec[:, 2:3] = s_c * g_c * alpha
    cvec[:, 3:4] = s_c * g_c * alpha * alpha
    cvec[:, 4:5] = s_c

    def js(h):
        return slice(h * hj, (h + 1) * hj)

    def same(h):
        rows = lax.broadcasted_iota(jnp.int32, (hj, height), 1) + x * height
        cols = lax.broadcasted_iota(jnp.int32, (hj, height), 0) + (col * wide + h * hj)
        return rows == cols

    def begin(h):
        ident = same(h)
        e = jnp.where(ident, 1.0, 0.0) - rvec[3:4] * acc[js(h)] * cvec[js(h), 4:5]
        eps_out[js(h)] = e
        m = (e * cvec[js(h), 0:1]).astype(BF)
        mixb[js(h)] = m
        rest = m.astype(F32) - jnp.where(ident, cvec[js(h), 1:2], 0.0)
        sbuf[js(h)] = (rest * rvec[2:3]).astype(BF)

    def product(h):
        return (rvec[1:2] * mixb[js(h)].astype(F32)) - rvec[3:4] * ybuf[js(h)]

    def middle(h):
        sq = product(h) - (rvec[3:4] * acc[js(h)]) * cvec[js(h), 2:3]
        square[js(h)] = sq
        m = sq.astype(BF)
        mixb[js(h)] = m
        a = cvec[js(h), 1:2]
        rest = m.astype(F32) - jnp.where(same(h), a * a, 0.0)
        sbuf[js(h)] = (rest * rvec[2:3]).astype(BF)

    def finish(h):
        cube = product(h) - (rvec[3:4] * acc[js(h)]) * cvec[js(h), 3:4]
        mixed = eps_out[js(h)] * cvec[js(h), 0:1]
        four = jnp.where(same(h), 4.0, 0.0)
        inv_out[js(h)] = rvec[0:1] * (four - 6.0 * mixed + 4.0 * square[js(h)] - cube)

    def q_part(h, q, d):
        rows = panel[pl.ds((2 * q + d) * czp, czp)].reshape(pp, height)
        return mm(sbuf[js(h)], rows, ((1,), (1,)))

    def hop(u, i, src, dst, right):
        return to(src, dst, x_s.at[u, i], x_r.at[u, i], row=xr if right else xl)

    def slot(u, i, right):
        return hop(u, i, qsend.at[u, i], qrecv.at[u, i], right)

    def quarter(u, q, d):
        return qfull.at[u, q, :, pl.ds(d * pp, pp)]

    def gathered(u, i, q, d, right):
        return hop(u, i, quarter(u, q, d), quarter(u, q, d), right)

    def stage1(u, h):
        for i, q, d, right in ((0, x2, 0, False), (1, x2, 1, True), (2, xl, 1, False), (3, xr, 0, True)):
            qsend[u, i] = q_part(h, q, d).astype(BF)
            slot(u, i, right).start()
        for i, q, d in ((0, xl, 0), (1, xr, 1), (2, x, 0), (3, x, 1)):
            keep[h, i] = q_part(h, q, d)

    def stage2(u, h):
        for i, right in ((0, False), (1, True)):
            slot(u, i, right).wait_recv()
            qsend[u, 4 + i] = (keep[h, i] + qrecv[u, i].astype(F32)).astype(BF)
            slot(u, 4 + i, right).start()

    def stage3(u, h):
        for i in (2, 3):
            slot(u, i, True).wait_recv()
        for d in (0, 1):
            slot(u, 4 + d, True).wait_recv()
            direct = qrecv[u, 3 - d].astype(F32)
            total = keep[h, 2 + d] + direct + qrecv[u, 4 + d].astype(F32)
            qfull[u, x, :, d * pp:(d + 1) * pp] = total.astype(BF)
            gathered(u, 6 + d, x, d, True).start()
            gathered(u, 8 + d, x, d, False).start()

    def add(u, h, q, first):
        term = mm(qfull[u, q], wpan[pl.ds(2 * q * czp, 2 * czp)].reshape(2 * pp, height), ((1,), (0,)))
        if first:
            ybuf[js(h)] = term
        else:
            ybuf[js(h)] += term

    def stage4(u, h):
        add(u, h, x, True)
        gathered(u, 6, xl, 0, True).wait_recv()
        gathered(u, 10, xl, 0, True).start()
        gathered(u, 9, xr, 1, False).wait_recv()
        gathered(u, 11, xr, 1, False).start()
        gathered(u, 7, xl, 1, True).wait_recv()
        add(u, h, xl, False)
        gathered(u, 8, xr, 0, False).wait_recv()
        add(u, h, xr, False)

    def stage5(u, h):
        gathered(u, 10, x2, 0, True).wait_recv()
        gathered(u, 11, x2, 1, False).wait_recv()
        add(u, h, x2, False)

    for h in (0, 1):
        begin(h)
        stage1(h, h)
    for stage in (stage2, stage3, stage4):
        for h in (0, 1):
            stage(h, h)
    for h in (0, 1):
        stage5(h, h)
        middle(h)
        stage1(2 + h, h)
    for stage in (stage2, stage3, stage4):
        for h in (0, 1):
            stage(2 + h, h)
    for h in (0, 1):
        stage5(2 + h, h)
        finish(h)

    for u in range(4):
        for i in range(6):
            slot(u, i, True).wait_send()
        for i in range(6, 12):
            gathered(u, i, x, 0, True).wait_send()

    def drain(d, s, subs):
        i, k = place(d, s)
        for j in subs:
            @pl.when((dist == 0) | (dist == (1 if d == 0 else 3)))
            def _():
                strip_hop(k, i, j, d, False).wait_send()

            @pl.when(dist == 0)
            def _():
                strip_hop(k, i, j, 1 - d, False).wait_send()

    def given(d, s):
        i, k = place(d, s)
        pair(k, core, i).wait_send()
        strip_pair(k, core, i).wait_send()

    def each(s, carry):
        for d in (0, 1):
            for j in range(SUBS):
                ring(d, s, j).wait_send()
            drain(d, s, range(SUBS))
            given(d, s)
        return carry

    drain(0, 0, range(SUBS))
    given(0, 0)
    lax.fori_loop(1, half, each, 0)
    for d in (0, 1):
        for j in subs_of(d, True):
            ring(d, half, j).wait_send()
        drain(d, half, subs_of(d, True))
    given(0, half)


def on_device(ncol, nrow, pair_density, band_pairs, valence, conduction, wave_vectors, momentum, guess_scale):
    ch, height = pair_density.shape
    pairs = ch * ncol
    nz = ncol // 2
    wide = height * nrow // ncol
    half = nz // 2
    places = 2 * (half + 1)
    hj = wide // 2
    pp = pairs // 8
    vm = pl.BlockSpec(memory_space=pltpu.VMEM)
    sm = pl.BlockSpec(memory_space=pltpu.SMEM)
    dma = pltpu.SemaphoreType.DMA
    out = jax.ShapeDtypeStruct((wide, height), F32)
    eps_t, inv_t = pl.pallas_call(
        functools.partial(kernel, ncol, nrow),
        out_shape=(out, out),
        in_specs=[pl.BlockSpec(memory_space=pl.ANY), vm, vm, vm, sm, sm, sm],
        out_specs=(vm, vm),
        scratch_shapes=[
            pltpu.VMEM((nz, 2, ch, height), BF),
            pltpu.VMEM((nz, 2, ch, height), BF),
            pltpu.VMEM((nz, 2, ch, 2 * wide), BF),
            pltpu.VMEM((pairs, 128), F32),
            pltpu.VMEM((wide, height), F32),
            pltpu.VMEM((8, height), F32),
            pltpu.VMEM((8, 2 * wide), F32),
            pltpu.VMEM((8, height), F32),
            pltpu.VMEM((wide, 128), F32),
            pltpu.VMEM((wide, height), BF),
            pltpu.VMEM((wide, height), BF),
            pltpu.VMEM((wide, height), F32),
            pltpu.VMEM((wide, height), F32),
            pltpu.VMEM((2, 4, hj, pp), F32),
            pltpu.VMEM((4, 6, hj, pp), BF),
            pltpu.VMEM((4, 6, hj, pp), BF),
            pltpu.VMEM((4, nrow, hj, 2 * pp), BF),
            dma((2, half, SUBS)),
            dma((2, half, SUBS)),
            dma((places,)),
            dma((places,)),
            dma((2, places, SUBS)),
            dma((places, SUBS)),
            dma((places,)),
            dma((places,)),
            dma(()),
            dma((places, SUBS)),
            dma((4, 12)),
            dma((4, 12)),
            pltpu.SemaphoreType.REGULAR,
            pltpu.SemaphoreType.REGULAR,
            pltpu.SemaphoreType.REGULAR,
        ],
        compiler_params=pltpu.CompilerParams(
            collective_id=0, has_side_effects=True, vmem_limit_bytes=44 * 1024 * 1024
        ),
        name="cohsex",
    )(pair_density, band_pairs, wave_vectors, guess_scale[None, :], valence, conduction, momentum)
    return eps_t.T, inv_t.T


def solution(mesh):
    placed = (P(("pb", "col"), "row"), P(), P(), P(), P(None, "pb"), P("pb"), P("pb"))
    return jax.shard_map(
        functools.partial(on_device, mesh.shape["col"], mesh.shape["row"]),
        mesh=mesh,
        in_specs=placed,
        out_specs=(P(("pb", "row"), "col"), P(("pb", "row"), "col")),
        check_vma=False,
    )
```

time: 151 us -> 148 us (0.980)
  other arithmetic: 5.9 us -> 0 us
  Pallas kernels: 137 us -> 139 us
    reduce_sum x3 -> x0, other arithmetic: 4.34 us -> none  [the longest x2 3.31 us: lookup(): return jnp.sum(jnp.where(picked, table[None, :], 0.0), axis=1)]
    unnamed x5 -> x16, local copies, waits for them, and re-layouts: 3.59 us -> 7.34 us
    pallas_call x1, Pallas kernels: 137 us -> 139 us  [on_device(): pl.pallas_call(functools.partial(kernel, ncol, nrow), out_shape=(out, out...]
    broadcast_in_dim x1 -> x0, local copies, waits for them, and re-layouts: 1.62 us -> none  [on_device(): jnp.broadcast_to(weight[:, None], (pairs, 128)).reshape(ncol, ch, 128)]
    another operation x2 -> x0, other arithmetic: 1.54 us -> none  [on_device(): both = jnp.stack([sqrt_all, guess_scale])]
where the time goes in v3:
time: 148 us; the launch traced here: 147 us
  Pallas kernels  139 us (94%)
  local copies, waits for them, and re-layouts  7.34 us (5%)
    pallas_call x1, Pallas kernels, on_device(): pl.pallas_call(functools.partial(kernel, ncol, nrow), out_shape=(out, out...  139 us
    unnamed x16, local copies, waits for them, and re-layouts  7.34 us

profile of v3, /device:TPU:40, one launch (start us, length us, event | category | flops | bytes accessed | tf_op | source)
XLA Modules:
  0.0 147.4 jit_solution(7063785217334248497)
XLA Ops:
  0.6 0.0 copy-start
  0.6 1.0 copy-done
  1.6 0.0 copy-start.1
  1.6 0.9 copy-done.1
  2.5 0.0 copy-start.2
  2.5 0.7 copy-done.2
  3.2 0.0 copy-start.3
  3.2 0.7 copy-done.3
  4.0 0.0 copy-start.4
  4.0 0.7 copy-done.4
  4.6 0.0 copy-start.5
  4.6 0.7 copy-done.5
  5.3 0.0 copy-start.6
  5.3 0.7 copy-done.6
  6.0 139.4 %cohsex.1 = (f32[192,1536]{1,0:T(8,128)S(1)}, f32[192,1536]{1,0:T(8,128)S(1)}) custom-call(bf16[96,1536]{1,0:T(8,128)(2,1)S(1)} %copy-done, s32[2,3072]{1,0:T(2,128)S(1)} %copy-done.2, s32[3,6144]{1,0:T(4,128)S(1)} %copy-done.1, f32[1,6144]{1,0:T(1,128)S(1)} %bitcast.5, f32[256]{0:T(256)S(1)} %copy-done.4, f32[12]{0:T(128)S(1)} %copy-done.5, f32[3]{0:T(128)S(1)} %copy-done.6), custom_call_target="tpu_custom_call" | custom-call | tf_op jit(solution)/shard_map/cohsex/pallas_call | solution.py:486
  145.4 1.0 copy.11
  146.4 1.0 copy.12
Async XLA Ops:
  0.6 1.0 copy-start
  1.6 0.9 copy-start.1
  2.5 0.7 copy-start.2
  3.2 0.7 copy-start.3
  4.0 0.7 copy-start.4
  4.6 0.7 copy-start.5
  5.3 0.7 copy-start.6

commit v4 on v2

--- a/solution.py
+++ b/solution.py
@@ -14,20 +14,15 @@
 SUBS = 2
 
 
-def lookup(indices, table):
-    levels = jnp.arange(table.shape[0], dtype=jnp.int32)
-    picked = indices[:, None] == levels[None, :]
-    return jnp.sum(jnp.where(picked, table[None, :], 0.0), axis=1)
-
-
 def mm(a, b, dims):
     return lax.dot_general(a, b, (dims, ((), ())), preferred_element_type=F32)
 
 
-def kernel(ncol, nrow, pd, weights, rowv, colv, eps_out, inv_out,
-           panel, wpan, strip, acc, chir, chic, rvec, cvec, sbuf, mixb, square, ybuf,
+def kernel(ncol, nrow, pd, bands_in, wave_in, scale_in, valence, conduction, momentum,
+           eps_out, inv_out,
+           bands, wave, scale, weights, panel, wpan, strip, acc, chir, chic, rvec, cvec, sbuf, mixb, square, ybuf,
            keep, qsend, qrecv, qfull,
-           ring_s, ring_r, pair_s, pair_r, sx_s, sx_r, sp_s, sp_r, own_s, loc_s, x_s, x_r):
+           in_s, ring_s, ring_r, pair_s, pair_r, sx_s, sx_r, sp_s, sp_r, own_s, loc_s, x_s, x_r):
     nz = ncol // 2
     half = nz // 2
     per = nz // nrow
@@ -55,6 +50,12 @@
             src_ref=src, dst_ref=dst, send_sem=ssem, recv_sem=rsem,
             device_id=where, device_id_type=MESH)
 
+    own = pltpu.make_async_copy(pd, panel.at[col], own_s)
+    own.start()
+    small = [pltpu.make_async_copy(a, b, in_s.at[i])
+             for i, (a, b) in enumerate(((bands_in, bands), (wave_in, wave), (scale_in, scale)))]
+    for copy in small:
+        copy.start()
     barrier = pltpu.get_barrier_semaphore()
     for where in (dict(col=up), dict(col=down), dict(col=mate), dict(row=xr), dict(row=xl)):
         pl.semaphore_signal(barrier, inc=1, device_id=where, device_id_type=MESH)
@@ -148,7 +149,7 @@
     def work(zi):
         w0 = 2 * zi
         rows = 2 * ch
-        wcol = weights[pl.ds(w0, 2)].reshape(rows, 128)
+        wcol = weights[pl.ds(pl.multiple_of(w0 * ch, 8), rows)]
         for t in range(height // 128):
             lanes = slice(t * 128, (t + 1) * 128)
             pf = panel[pl.ds(w0, 2), :, lanes].reshape(rows, 128).astype(F32)
@@ -164,17 +165,27 @@
         mine = jnp.where(core == 0, both[:, :wide].astype(F32), both[:, wide:].astype(F32)).astype(BF)
         acc[...] += mm(mine, wpan[pl.ds(w0, 2)].reshape(rows, height), ((0,), (0,)))
 
-    own = pltpu.make_async_copy(pd, panel.at[col], own_s)
-    own.start()
-    acc[...] = jnp.zeros_like(acc)
-    chir[...] = jnp.zeros_like(chir)
-    chic[...] = jnp.zeros_like(chic)
     own.wait()
     for j in range(SUBS):
         ring(0, 1, j).start()
         ring(1, 1, j).start()
     for j in range(SUBS):
         arrived(0, 0, j)
+    acc[...] = jnp.zeros_like(acc)
+    chir[...] = jnp.zeros_like(chir)
+    chic[...] = jnp.zeros_like(chic)
+    for copy in small:
+        copy.wait()
+
+    def look(ids, table):
+        def level(v, found):
+            return jnp.where(ids == v, table[v], found)
+        return lax.fori_loop(0, table.shape[0], level, jnp.zeros(ids.shape, F32), unroll=4)
+
+    weight = 4.0 / (look(bands[0:1], valence) - look(bands[1:2], conduction))
+    for t in range(weights.shape[0] // 128):
+        lanes = slice(t * 128, (t + 1) * 128)
+        weights[lanes] = jnp.broadcast_to(weight[:, lanes], (128, 128)).T
 
     def subs_of(d, last):
         if not last:
@@ -248,19 +259,33 @@
     tail(half - 1, False)
     tail(half, True)
 
-    s_r = rowv[0:1]
+    def root(first, count):
+        lanes = pl.ds(pl.multiple_of(first, 128), count)
+        total = jnp.zeros((1, count), F32)
+        for i in range(3):
+            shifted = wave[i:i + 1, lanes].astype(F32) + momentum[i]
+            total = total + shifted * shifted
+        return jnp.sqrt(4.0 * math.pi / total), scale[:, lanes]
+
+    s_r, t_r = root(x * height, height)
     chi_r = jnp.sum(chir[...], axis=0, keepdims=True)
     diag_r = 1.0 - s_r * chi_r * s_r
-    g_r = rowv[1:2] / diag_r
+    g_r = t_r / diag_r
     m_r = diag_r * g_r
     rvec[0:1] = g_r
     rvec[1:2] = g_r + (m_r.astype(BF).astype(F32) - m_r)
     rvec[2:3] = s_r * g_r
-    chi_t = jnp.broadcast_to(jnp.sum(chic[...], axis=0, keepdims=True), chic.shape).T
-    chi_c = jnp.where(core == 0, chi_t[:wide, 0:1], chi_t[wide:, 0:1])
-    s_c = colv[:, 0:1]
-    diag_c = 1.0 - s_c * chi_c * s_c
-    g_c = colv[:, 1:2] / diag_c
+    rvec[3:4] = s_r
+    s_l, t_l = root(z * chip_wide, chip_wide)
+    chi_l = jnp.sum(chic[...], axis=0, keepdims=True)
+    chic[0:1] = s_l
+    chic[1:2] = t_l
+    chic[2:3] = chi_l
+    turned = chic[...].T
+    turned = jnp.where(core == 0, turned[:wide], turned[wide:])
+    s_c = turned[:, 0:1]
+    diag_c = 1.0 - s_c * turned[:, 2:3] * s_c
+    g_c = turned[:, 1:2] / diag_c
     alpha = (diag_c * g_c).astype(BF).astype(F32)
     cvec[:, 0:1] = g_c
     cvec[:, 1:2] = alpha
@@ -278,7 +303,7 @@
 
     def begin(h):
         ident = same(h)
-        e = jnp.where(ident, 1.0, 0.0) - rowv[0:1] * acc[js(h)] * cvec[js(h), 4:5]
+        e = jnp.where(ident, 1.0, 0.0) - rvec[3:4] * acc[js(h)] * cvec[js(h), 4:5]
         eps_out[js(h)] = e
         m = (e * cvec[js(h), 0:1]).astype(BF)
         mixb[js(h)] = m
@@ -286,10 +311,10 @@
         sbuf[js(h)] = (rest * rvec[2:3]).astype(BF)
 
     def product(h):
-        return (rvec[1:2] * mixb[js(h)].astype(F32)) - rowv[0:1] * ybuf[js(h)]
+        return (rvec[1:2] * mixb[js(h)].astype(F32)) - rvec[3:4] * ybuf[js(h)]
 
     def middle(h):
-        sq = product(h) - (rowv[0:1] * acc[js(h)]) * cvec[js(h), 2:3]
+        sq = product(h) - (rvec[3:4] * acc[js(h)]) * cvec[js(h), 2:3]
         square[js(h)] = sq
         m = sq.astype(BF)
         mixb[js(h)] = m
@@ -298,7 +323,7 @@
         sbuf[js(h)] = (rest * rvec[2:3]).astype(BF)
 
     def finish(h):
-        cube = product(h) - (rowv[0:1] * acc[js(h)]) * cvec[js(h), 3:4]
+        cube = product(h) - (rvec[3:4] * acc[js(h)]) * cvec[js(h), 3:4]
         mixed = eps_out[js(h)] * cvec[js(h), 0:1]
         four = jnp.where(same(h), 4.0, 0.0)
         inv_out[js(h)] = rvec[0:1] * (four - 6.0 * mixed + 4.0 * square[js(h)] - cube)
@@ -323,6 +348,8 @@
         for i, q, d, right in ((0, x2, 0, False), (1, x2, 1, True), (2, xl, 1, False), (3, xr, 0, True)):
             qsend[u, i] = q_part(h, q, d).astype(BF)
             slot(u, i, right).start()
+
+    def stage1_kept(h):
         for i, q, d in ((0, xl, 0), (1, xr, 1), (2, x, 0), (3, x, 1)):
             keep[h, i] = q_part(h, q, d)
 
@@ -369,6 +396,8 @@
     for h in (0, 1):
         begin(h)
         stage1(h, h)
+    for h in (0, 1):
+        stage1_kept(h)
     for stage in (stage2, stage3, stage4):
         for h in (0, 1):
             stage(h, h)
@@ -376,6 +405,8 @@
         stage5(h, h)
         middle(h)
         stage1(2 + h, h)
+    for h in (0, 1):
+        stage1_kept(h)
     for stage in (stage2, stage3, stage4):
         for h in (0, 1):
             stage(2 + h, h)
@@ -419,31 +450,29 @@
 
 
 def on_device(ncol, nrow, pair_density, band_pairs, valence, conduction, wave_vectors, momentum, guess_scale):
-    column_index = lax.axis_index("col")
-    row_index = lax.axis_index("row")
     ch, height = pair_density.shape
     pairs = ch * ncol
     wide = height * nrow // ncol
-    weight = 4.0 / (lookup(band_pairs[0], valence) - lookup(band_pairs[1], conduction))
-    weights = jnp.broadcast_to(weight[:, None], (pairs, 128)).reshape(ncol, ch, 128)
-    shifted = wave_vectors.astype(F32) + momentum[:, None]
-    sqrt_all = jnp.sqrt(4.0 * math.pi / jnp.sum(shifted * shifted, axis=0))
-    both = jnp.stack([sqrt_all, guess_scale])
-    rowv = jnp.pad(lax.dynamic_slice_in_dim(both, row_index * height, height, 1), ((0, 6), (0, 0)))
-    colv = jnp.pad(lax.dynamic_slice_in_dim(both, column_index * wide, wide, 1).T, ((0, 0), (0, 126)))
+    scales = guess_scale[None, :]
     half = ncol // 4
     places = 2 * (half + 1)
     hj = wide // 2
     pp = pairs // 8
     vm = pl.BlockSpec(memory_space=pltpu.VMEM)
+    sm = pl.BlockSpec(memory_space=pltpu.SMEM)
+    hbm = pl.BlockSpec(memory_space=pltpu.HBM)
     dma = pltpu.SemaphoreType.DMA
     out = jax.ShapeDtypeStruct((wide, height), F32)
     eps_t, inv_t = pl.pallas_call(
         functools.partial(kernel, ncol, nrow),
-        out_shape=(out, out),
-        in_specs=[vm] * 4,
+        out_shape=(pltpu.VMEM((wide, height), F32), pltpu.VMEM((wide, height), F32)),
+        in_specs=[hbm, hbm, hbm, hbm, sm, sm, sm],
         out_specs=(vm, vm),
         scratch_shapes=[
+            pltpu.VMEM(band_pairs.shape, jnp.int32),
+            pltpu.VMEM(wave_vectors.shape, jnp.int32),
+            pltpu.VMEM(scales.shape, F32),
+            pltpu.VMEM((pairs, 128), F32),
             pltpu.VMEM((ncol, ch, height), BF),
             pltpu.VMEM((ncol, ch, height), BF),
             pltpu.VMEM((ncol, ch, 2 * wide), BF),
@@ -460,6 +489,7 @@
             pltpu.VMEM((4, 6, hj, pp), BF),
             pltpu.VMEM((4, 6, hj, pp), BF),
             pltpu.VMEM((4, nrow, hj, 2 * pp), BF),
+            dma((3,)),
             dma((2, half, SUBS)),
             dma((2, half, SUBS)),
             dma((places, SUBS)),
@@ -477,7 +507,7 @@
             collective_id=0, has_side_effects=True, vmem_limit_bytes=60 * 1024 * 1024
         ),
         name="cohsex",
-    )(pair_density, weights, rowv, colv)
+    )(pair_density, band_pairs, wave_vectors, scales, valence, conduction, momentum)
     return eps_t.T, inv_t.T
 
 

time: 151 us -> 137 us (0.907)
  other arithmetic: 5.9 us -> 0 us
  local copies, waits for them, and re-layouts: 7.4 us -> 2.03 us
  Pallas kernels: 137 us -> 134 us
    reduce_sum x3 -> x0, other arithmetic: 4.34 us -> none  [the longest x2 3.31 us: lookup(): return jnp.sum(jnp.where(picked, table[None, :], 0.0), axis=1)]
    pallas_call x1, Pallas kernels: 137 us -> 134 us  [on_device(): pl.pallas_call(functools.partial(kernel, ncol, nrow), out_shape=(pltpu.VM...]
    broadcast_in_dim x1 -> x0, local copies, waits for them, and re-layouts: 1.62 us -> none  [on_device(): jnp.broadcast_to(weight[:, None], (pairs, 128)).reshape(ncol, ch, 128)]
    unnamed x5 -> x2, local copies, waits for them, and re-layouts: 3.59 us -> 2.03 us
    another operation x2 -> x0, other arithmetic: 1.54 us -> none  [on_device(): both = jnp.stack([sqrt_all, guess_scale])]
where the time goes in v4:
time: 137 us
  Pallas kernels  134 us (98%)
  local copies, waits for them, and re-layouts  2.03 us (1%)
    pallas_call x1, Pallas kernels, on_device(): pl.pallas_call(functools.partial(kernel, ncol, nrow), out_shape=(pltpu.VM...  134 us

profile of v4, /device:TPU:40, one launch (start us, length us, event | category | flops | bytes accessed | tf_op | source)
XLA Modules:
  0.0 137.1 jit_solution(10047518077556307000)
XLA Ops:
  0.6 134.4 %cohsex.1 = (f32[192,1536]{1,0:T(8,128)S(1)}, f32[192,1536]{1,0:T(8,128)S(1)}) custom-call(bf16[96,1536]{1,0:T(8,128)(2,1)} %pd.1, s32[2,3072]{1,0:T(2,128)} %bands_in.1, s32[3,6144]{1,0:T(4,128)} %wave_in.1, f32[1,6144]{1,0:T(1,128)} %bitcast.5, f32[256]{0:T(256)} %valence.1, f32[12]{0:T(128)} %conduction.1, f32[3]{0:T(128)} %momentum.1), custom_call_target="tpu_custom_call" | custom-call | tf_op jit(solution)/shard_map/cohsex/pallas_call | solution.py:466
  135.1 1.0 copy.11
  136.1 1.0 copy.12

commit v5 on v4

--- a/solution.py
+++ b/solution.py
@@ -18,9 +18,9 @@
     return lax.dot_general(a, b, (dims, ((), ())), preferred_element_type=F32)
 
 
-def kernel(ncol, nrow, pd, bands_in, wave_in, scale_in, valence, conduction, momentum,
+def kernel(ncol, nrow, pd, bands_in, wave_in, scale_in, valence_in, conduction_in, momentum_in,
            eps_out, inv_out,
-           bands, wave, scale, weights, panel, wpan, strip, acc, chir, chic, rvec, cvec, sbuf, mixb, square, ybuf,
+           bands, wave, scale, valence, conduction, momentum, weights, panel, wpan, strip, acc, chir, chic, rvec, cvec, sbuf, mixb, square, ybuf,
            keep, qsend, qrecv, qfull,
            in_s, ring_s, ring_r, pair_s, pair_r, sx_s, sx_r, sp_s, sp_r, own_s, loc_s, x_s, x_r):
     nz = ncol // 2
@@ -53,7 +53,9 @@
     own = pltpu.make_async_copy(pd, panel.at[col], own_s)
     own.start()
     small = [pltpu.make_async_copy(a, b, in_s.at[i])
-             for i, (a, b) in enumerate(((bands_in, bands), (wave_in, wave), (scale_in, scale)))]
+             for i, (a, b) in enumerate((
+                 (bands_in, bands), (wave_in, wave), (scale_in, scale), (valence_in, valence),
+                 (conduction_in, conduction), (momentum_in, momentum)))]
     for copy in small:
         copy.start()
     barrier = pltpu.get_barrier_semaphore()
@@ -136,17 +138,27 @@
         def _():
             strip_pair_on(k, i, j).start()
 
+    def ready_panel(d, s, j):
+        i, k = place(d, s)
+        pair(k + 1 - 2 * core, i, j).wait_recv()
+
+    def ready_strip(d, s, j):
+        i, k = place(d, s)
+        strip_pair_on(k + 1 - 2 * core, i, j).wait_recv()
+
+        @pl.when(dist == 0)
+        def _():
+            strip_local(k, i, j).wait()
+
     def ready(d, s, j):
-        i, k = place(d, s)
-        km = k + 1 - 2 * core
-        pair(km, i, j).wait_recv()
-        strip_pair_on(km, i, j).wait_recv()
-
-        @pl.when(dist == 0)
-        def _():
-            strip_local(k, i, j).wait()
+        ready_panel(d, s, j)
+        ready_strip(d, s, j)
 
     def work(zi):
+        spread(zi)
+        gain(zi)
+
+    def spread(zi):
         w0 = 2 * zi
         rows = 2 * ch
         wcol = weights[pl.ds(pl.multiple_of(w0 * ch, 8), rows)]
@@ -156,6 +168,11 @@
             wb = (pf * wcol).astype(BF)
             wpan[pl.ds(w0, 2), :, lanes] = wb.reshape(2, ch, 128)
             chir[:, lanes] += (wb.astype(F32) * pf).reshape(rows // 8, 8, 128).sum(0)
+
+    def gain(zi):
+        w0 = 2 * zi
+        rows = 2 * ch
+        wcol = weights[pl.ds(pl.multiple_of(w0 * ch, 8), rows)]
         for t in range(chip_wide // 128):
             lanes = slice(t * 128, (t + 1) * 128)
             sf = strip[pl.ds(w0, 2), :, lanes].reshape(rows, 128).astype(F32)
@@ -171,21 +188,6 @@
         ring(1, 1, j).start()
     for j in range(SUBS):
         arrived(0, 0, j)
-    acc[...] = jnp.zeros_like(acc)
-    chir[...] = jnp.zeros_like(chir)
-    chic[...] = jnp.zeros_like(chic)
-    for copy in small:
-        copy.wait()
-
-    def look(ids, table):
-        def level(v, found):
-            return jnp.where(ids == v, table[v], found)
-        return lax.fori_loop(0, table.shape[0], level, jnp.zeros(ids.shape, F32), unroll=4)
-
-    weight = 4.0 / (look(bands[0:1], valence) - look(bands[1:2], conduction))
-    for t in range(weights.shape[0] // 128):
-        lanes = slice(t * 128, (t + 1) * 128)
-        weights[lanes] = jnp.broadcast_to(weight[:, lanes], (128, 128)).T
 
     def subs_of(d, last):
         if not last:
@@ -215,6 +217,26 @@
                     ready(d, s, j)
 
     bring(1, False, False)
+    acc[...] = jnp.zeros_like(acc)
+    chir[...] = jnp.zeros_like(chir)
+    chic[...] = jnp.zeros_like(chic)
+    for copy in small:
+        copy.wait()
+
+    def look(ids, table):
+        def level(v, found):
+            return jnp.where(ids == v, table[v], found)
+        return lax.fori_loop(0, table.shape[0], level, jnp.zeros(ids.shape, F32), unroll=4)
+
+    tiles = weights.shape[0] // 128
+
+    def stacked(i):
+        return jnp.concatenate([bands[i:i + 1, t * 128:(t + 1) * 128] for t in range(tiles)], axis=0)
+
+    weight = 4.0 / (look(stacked(0), valence) - look(stacked(1), conduction))
+    for t in range(tiles):
+        weights[t * 128:(t + 1) * 128] = jnp.broadcast_to(weight[t:t + 1], (128, 128)).T
+
     for j in range(SUBS):
         strip_step(0, 0, j)
 
@@ -241,23 +263,40 @@
         return carry
 
     lax.fori_loop(2, half - 1, early, 0)
-    def tail(s, final):
-        settle(s, final)
+    def tail(s):
+        settle(s, False)
 
         def each(d, c):
             work(chunk_of(d, s) // 2)
             return c
-        lax.fori_loop(0, 1 if final else 2, each, 0)
+        lax.fori_loop(0, 2, each, 0)
 
     bring(half - 1, True, False)
     relay(half - 2, False)
-    tail(half - 3, False)
+    tail(half - 3)
     bring(half, False, True)
     relay(half - 1, False)
-    tail(half - 2, False)
-    relay(half, True)
-    tail(half - 1, False)
-    tail(half, True)
+    tail(half - 2)
+
+    @pl.when(dist != 2)
+    def _():
+        relay(half, True)
+
+    tail(half - 1)
+    far = chunk_of(0, half) // 2
+    for d in (0, 1):
+        for j in subs_of(d, True):
+            ready_panel(d, half, j)
+    spread(far)
+
+    @pl.when(dist == 2)
+    def _():
+        relay(half, True)
+
+    for d in (0, 1):
+        for j in subs_of(d, True):
+            ready_strip(d, half, j)
+    gain(far)
 
     def root(first, count):
         lanes = pl.ds(pl.multiple_of(first, 128), count)
@@ -349,8 +388,9 @@
             qsend[u, i] = q_part(h, q, d).astype(BF)
             slot(u, i, right).start()
 
-    def stage1_kept(h):
-        for i, q, d in ((0, xl, 0), (1, xr, 1), (2, x, 0), (3, x, 1)):
+    def kept(h, which):
+        parts = ((0, xl, 0), (1, xr, 1)) if which == 0 else ((2, x, 0), (3, x, 1))
+        for i, q, d in parts:
             keep[h, i] = q_part(h, q, d)
 
     def stage2(u, h):
@@ -377,42 +417,56 @@
         else:
             ybuf[js(h)] += term
 
-    def stage4(u, h):
-        add(u, h, x, True)
+    def forward(u):
         gathered(u, 6, xl, 0, True).wait_recv()
         gathered(u, 10, xl, 0, True).start()
         gathered(u, 9, xr, 1, False).wait_recv()
         gathered(u, 11, xr, 1, False).start()
+
+    def add_near(u, h):
         gathered(u, 7, xl, 1, True).wait_recv()
         add(u, h, xl, False)
         gathered(u, 8, xr, 0, False).wait_recv()
         add(u, h, xr, False)
 
-    def stage5(u, h):
+    def add_far(u, h):
         gathered(u, 10, x2, 0, True).wait_recv()
         gathered(u, 11, x2, 1, False).wait_recv()
         add(u, h, x2, False)
 
-    for h in (0, 1):
-        begin(h)
-        stage1(h, h)
-    for h in (0, 1):
-        stage1_kept(h)
-    for stage in (stage2, stage3, stage4):
-        for h in (0, 1):
-            stage(h, h)
-    for h in (0, 1):
-        stage5(h, h)
-        middle(h)
-        stage1(2 + h, h)
-    for h in (0, 1):
-        stage1_kept(h)
-    for stage in (stage2, stage3, stage4):
-        for h in (0, 1):
-            stage(2 + h, h)
-    for h in (0, 1):
-        stage5(2 + h, h)
-        finish(h)
+    def exchange(u):
+        stage2(u, 0)
+        kept(1, 0)
+        stage2(u + 1, 1)
+        kept(0, 1)
+        stage3(u, 0)
+        kept(1, 1)
+        stage3(u + 1, 1)
+        add(u, 0, x, True)
+        forward(u)
+        add(u + 1, 1, x, True)
+        add_near(u, 0)
+        forward(u + 1)
+        add_far(u, 0)
+
+    begin(0)
+    stage1(0, 0)
+    begin(1)
+    stage1(1, 1)
+    kept(0, 0)
+    exchange(0)
+    middle(0)
+    stage1(2, 0)
+    add_near(1, 1)
+    add_far(1, 1)
+    middle(1)
+    stage1(3, 1)
+    kept(0, 0)
+    exchange(2)
+    finish(0)
+    add_near(3, 1)
+    add_far(3, 1)
+    finish(1)
 
     for u in range(4):
         for i in range(6):
@@ -459,19 +513,21 @@
     hj = wide // 2
     pp = pairs // 8
     vm = pl.BlockSpec(memory_space=pltpu.VMEM)
-    sm = pl.BlockSpec(memory_space=pltpu.SMEM)
     hbm = pl.BlockSpec(memory_space=pltpu.HBM)
     dma = pltpu.SemaphoreType.DMA
     out = jax.ShapeDtypeStruct((wide, height), F32)
     eps_t, inv_t = pl.pallas_call(
         functools.partial(kernel, ncol, nrow),
         out_shape=(pltpu.VMEM((wide, height), F32), pltpu.VMEM((wide, height), F32)),
-        in_specs=[hbm, hbm, hbm, hbm, sm, sm, sm],
+        in_specs=[hbm] * 7,
         out_specs=(vm, vm),
         scratch_shapes=[
             pltpu.VMEM(band_pairs.shape, jnp.int32),
             pltpu.VMEM(wave_vectors.shape, jnp.int32),
             pltpu.VMEM(scales.shape, F32),
+            pltpu.SMEM(valence.shape, F32),
+            pltpu.SMEM(conduction.shape, F32),
+            pltpu.SMEM(momentum.shape, F32),
             pltpu.VMEM((pairs, 128), F32),
             pltpu.VMEM((ncol, ch, height), BF),
             pltpu.VMEM((ncol, ch, height), BF),
@@ -489,7 +545,7 @@
             pltpu.VMEM((4, 6, hj, pp), BF),
             pltpu.VMEM((4, 6, hj, pp), BF),
             pltpu.VMEM((4, nrow, hj, 2 * pp), BF),
-            dma((3,)),
+            dma((6,)),
             dma((2, half, SUBS)),
             dma((2, half, SUBS)),
             dma((places, SUBS)),

time: 137 us -> 136 us (level)
  no operation moved by 1% of the time
where the time goes in v5:
time: 136 us
  Pallas kernels  134 us (99%)
  local copies, waits for them, and re-layouts  2.03 us (1%)
    pallas_call x1, Pallas kernels, on_device(): pl.pallas_call(functools.partial(kernel, ncol, nrow), out_shape=(pltpu.VM...  134 us

profile of v5, /device:TPU:40, one launch (start us, length us, event | category | flops | bytes accessed | tf_op | source)
XLA Modules:
  0.0 136.2 jit_solution(4428023550546868295)
XLA Ops:
  0.6 133.5 %cohsex.1 = (f32[192,1536]{1,0:T(8,128)S(1)}, f32[192,1536]{1,0:T(8,128)S(1)}) custom-call(bf16[96,1536]{1,0:T(8,128)(2,1)} %pd.1, s32[2,3072]{1,0:T(2,128)} %bands_in.1, s32[3,6144]{1,0:T(4,128)} %wave_in.1, f32[1,6144]{1,0:T(1,128)} %bitcast.5, f32[256]{0:T(256)} %valence_in.1, f32[12]{0:T(128)} %conduction_in.1, f32[3]{0:T(128)} %momentum_in.1), custom_call_target="tpu_custom_call" | custom-call | tf_op jit(solution)/shard_map/cohsex/pallas_call | solution.py:519
  134.2 1.0 copy.11
  135.2 1.0 copy.12

commit v6 on v5

--- a/solution.py
+++ b/solution.py
@@ -407,8 +407,9 @@
             direct = qrecv[u, 3 - d].astype(F32)
             total = keep[h, 2 + d] + direct + qrecv[u, 4 + d].astype(F32)
             qfull[u, x, :, d * pp:(d + 1) * pp] = total.astype(BF)
-            gathered(u, 6 + d, x, d, True).start()
-            gathered(u, 8 + d, x, d, False).start()
+            gathered(u, 6 if d == 0 else 9, x, d, d == 0).start()
+        gathered(u, 7, x, 1, True).start()
+        gathered(u, 8, x, 0, False).start()
 
     def add(u, h, q, first):
         term = mm(qfull[u, q], wpan[pl.ds(2 * q * cpp, 2 * cpp)].reshape(2 * pp, height), ((1,), (0,)))

time: 136 us -> 136 us (level)
  no operation moved by 1% of the time
where the time goes in v6:
time: 136 us
  Pallas kernels  134 us (99%)
  local copies, waits for them, and re-layouts  2.03 us (1%)
    pallas_call x1, Pallas kernels, on_device(): pl.pallas_call(functools.partial(kernel, ncol, nrow), out_shape=(pltpu.VM...  134 us

profile of v6, /device:TPU:40, one launch (start us, length us, event | category | flops | bytes accessed | tf_op | source)
XLA Modules:
  0.0 136.3 jit_solution(6156571825056709452)
XLA Ops:
  0.6 133.6 %cohsex.1 = (f32[192,1536]{1,0:T(8,128)S(1)}, f32[192,1536]{1,0:T(8,128)S(1)}) custom-call(bf16[96,1536]{1,0:T(8,128)(2,1)} %pd.1, s32[2,3072]{1,0:T(2,128)} %bands_in.1, s32[3,6144]{1,0:T(4,128)} %wave_in.1, f32[1,6144]{1,0:T(1,128)} %bitcast.5, f32[256]{0:T(256)} %valence_in.1, f32[12]{0:T(128)} %conduction_in.1, f32[3]{0:T(128)} %momentum_in.1), custom_call_target="tpu_custom_call" | custom-call | tf_op jit(solution)/shard_map/cohsex/pallas_call | solution.py:520
  134.2 1.0 copy.11
  135.2 1.0 copy.12
